TPU v7x, 512 devices: a whole 4x8x8 slice. The times are simulated.
512 devices in a mesh: rng: 8 (over z), az: 64 (over y, x, core).
Axes of the slice: x: 4, y: 8, z: 8, core: 2. Of those that a mesh axis runs over, the one named last changes fastest.
Arguments:
- spectrum: float32 [4096, 2, 32768], P('rng', None, 'az'), may hold values from -9 to 9
- src_block: int32 [256, 32], P('az', 'rng'), may hold values from 0 to 30, as said below
- offsets: int32 [256, 4096], P('az', 'rng'), may hold values from 0 to 127
- tap_weights: float32 [8, 256, 4096], P(None, 'az', 'rng'), may hold values from -2 to 2
Outputs:
- image: float32 [4096, 2, 32768], P(('rng', 'az'))
Inputs may be any that keep to these rules, and one draw needn't show every extreme that they name: src_block[g, b] lies between min(b, 30) and min(b + 5, 30); a shift of 5 blocks occurs in every draw.
All inputs are finite; a program needn't handle non-finite values.
Results may differ from a plain program's by a relative error of at most 0.00007.
Values sent between devices are 32-bit elements; how exact they have to be, the bound alone decides.
No kernel may reach another device: no remote copies, remote signals or barrier semaphores. Data moves between devices by JAX's collectives and lax.ppermute only.
A program may use at most 128 MiB of HBM per device.

v0:
```python
import math

import jax
import jax.numpy as jnp
from jax import lax
from jax.sharding import Mesh
from jax.sharding import PartitionSpec as P

AZ1 = 128
BLOCK = 128
GW = 128
TAPS = 8
SHIFT_B = 5
AZ = ("az_0", "az_1", "az_2")
RNG_AZ = ("rng", "az_0", "az_1", "az_2")


def from_behind(shard, axis, by):
    peers = lax.axis_size(axis)
    pairs = [(i, i + by) for i in range(peers) if 0 <= i + by < peers]
    return lax.ppermute(shard, axis, pairs)


def by_axis(shard, axes):
    for axis in axes:
        shard = lax.psum(shard, axis)
    return shard


def roots(first_count, second_count, modulus):
    product = (
        jnp.arange(first_count, dtype=jnp.int32)[:, None]
        * jnp.arange(second_count, dtype=jnp.int32)[None, :]
        % modulus
    )
    angles = product.astype(jnp.float32) * (2.0 * math.pi / modulus)
    return (jnp.cos(angles), jnp.sin(angles))


def inverse_rows(block_in):
    rows_here = block_in.shape[1]
    total_len = block_in.shape[3]
    first_len = AZ1
    second_len = total_len // first_len
    highest = lax.Precision.HIGHEST
    real_part = block_in[0, :, 0].reshape(rows_here, first_len, second_len)
    imag_part = block_in[0, :, 1].reshape(rows_here, first_len, second_len)
    first_cos, first_sin = roots(first_len, first_len, first_len)
    step_real = jnp.einsum("an,rnm->ram", first_cos, real_part, precision=highest) - jnp.einsum(
        "an,rnm->ram", first_sin, imag_part, precision=highest
    )
    step_imag = jnp.einsum("an,rnm->ram", first_cos, imag_part, precision=highest) + jnp.einsum(
        "an,rnm->ram", first_sin, real_part, precision=highest
    )
    twist_cos, twist_sin = roots(first_len, second_len, total_len)
    turned_real = step_real * twist_cos - step_imag * twist_sin
    turned_imag = step_real * twist_sin + step_imag * twist_cos
    second_cos, second_sin = roots(second_len, second_len, second_len)
    final_real = jnp.einsum("rbn,cn->rbc", turned_real, second_cos, precision=highest) - jnp.einsum(
        "rbn,cn->rbc", turned_imag, second_sin, precision=highest
    )
    final_imag = jnp.einsum("rbn,cn->rbc", turned_real, second_sin, precision=highest) + jnp.einsum(
        "rbn,cn->rbc", turned_imag, second_cos, precision=highest
    )
    final_real = final_real.transpose(0, 2, 1).reshape(rows_here, total_len) / total_len
    final_imag = final_imag.transpose(0, 2, 1).reshape(rows_here, total_len) / total_len
    return jnp.stack([final_real, final_imag], axis=1)[None]


def apply_taps(flat, flat_rows, weights):
    result = jnp.zeros((weights.shape[1], weights.shape[2], flat.shape[1]), jnp.float32)
    for tap_index in range(TAPS):
        result = result + weights[tap_index][:, :, None] * jnp.take(
            flat, flat_rows + tap_index, axis=0
        )
    return result


def body(spectrum, src_block, offsets, tap_weights):
    rows_dev = spectrum.shape[0]
    columns = spectrum.shape[2]
    groups = columns // GW
    blocks_dev = rows_dev // BLOCK
    reach_blocks = SHIFT_B + 1
    depth = (reach_blocks + blocks_dev - 1) // blocks_dev
    rng_count = lax.axis_size("rng")
    az_count = lax.axis_size(AZ)
    position = lax.axis_index("rng")
    total_rows = rows_dev * rng_count
    rows_after = rows_dev // az_count
    total_cells = total_rows * columns * az_count
    local = (
        spectrum.reshape(rows_dev, 2, groups, GW)
        .transpose(2, 0, 1, 3)
        .reshape(groups, rows_dev, 2 * GW)
    )
    gathered = [local]
    for distance in range(1, depth + 1):
        needed = min(blocks_dev, reach_blocks - (distance - 1) * blocks_dev) * BLOCK
        gathered.append(from_behind(local[:, :needed], "rng", -distance))
    extended = jnp.concatenate(gathered, axis=1)
    ext_rows = extended.shape[1]
    flat = extended.reshape(groups * ext_rows, 2 * GW)
    local_src = (src_block - position * blocks_dev) * BLOCK
    src_rows = (local_src[:, :, None] + offsets.reshape(groups, blocks_dev, BLOCK)).reshape(
        groups, rows_dev
    )
    flat_rows = jnp.arange(groups, dtype=jnp.int32)[:, None] * ext_rows + src_rows
    remapped = apply_taps(flat, flat_rows, tap_weights)
    ordered = (
        remapped.reshape(groups, rows_dev, 2, GW)
        .transpose(1, 2, 0, 3)
        .reshape(az_count, rows_after, 2, columns)
    )
    band = inverse_rows(lax.all_to_all(ordered, AZ, split_axis=0, concat_axis=3, tiled=True))
    band = band.reshape(rows_after, 2, columns * az_count)
    energy = by_axis(jnp.sum(band * band), RNG_AZ)
    scaling = lax.rsqrt(energy / total_cells + 1e-06)
    return band * scaling


def solution(mesh):
    torus = Mesh(mesh.devices.reshape(mesh.shape["rng"], 8, 4, 2), ("rng", "az_0", "az_1", "az_2"))
    placed = (P("rng", None, AZ), P(AZ, "rng"), P(AZ, "rng"), P(None, AZ, "rng"))
    return jax.shard_map(
        body, mesh=torus, in_specs=placed, out_specs=P(RNG_AZ, None, None), check_vma=False
    )
```

profile of v0, /device:TPU:1, one launch (start us, length us, event | category | flops | bytes accessed | tf_op | source)
XLA Modules:
  0.0 360.9 jit_solution(4342414353455732580)
XLA Ops:
  0.0 3.3 reshape.99
  5.7 2.9 reshape.100
  13.1 92.6 %collective-permute-done.1 = f32[4,256,256]{2,1,0:T(8,128)S(1)} collective-permute-done((f32[4,256,256]{2,1,0:T(8,128)}, f32[4,256,256]{2,1,0:T(8,128)S(1)}, u32[]{:S(2)}, u32[]{:S(2)}) %collective-permute-start.1) | collective-permute-done | bytes 1048608 | tf_op jit(solution)/shard_map/ppermute | solution.py:21
  105.7 4.3 %pad_maximum_fusion = f32[4,1280,256]{2,1,0:T(8,128)} fusion(f32[4,256,256]{2,1,0:T(8,128)S(1)} %collective-permute-done.1, f32[4,512,256]{2,1,0:T(8,128)} %collective-permute-done, f32[4,512,256]{2,1,0:T(8,128)S(1)} %reshape.100), kind=kLoop, calls=%fused_computation.8 | loop fusion | flops 2621440 | bytes 10485760 | tf_op jit(solution)/shard_map/concatenate | solution.py:101
  110.0 9.1 %gather_fusion = f32[2048,256]{1,0:T(8,128)S(1)} fusion(f32[5120,256]{1,0:T(8,128)} %bitcast.113, s32[2048]{0:T(1024)S(1)} %broadcast_clamp_fusion.7), kind=kCustom, calls=%fused_computation.clone | custom fusion | bytes 4202496 | tf_op jit(solution)/shard_map/jit(_take)/gather | solution.py:73
  120.9 9.1 %gather_fusion.1 = f32[2048,256]{1,0:T(8,128)S(1)} fusion(f32[5120,256]{1,0:T(8,128)} %bitcast.114, s32[2048]{0:T(1024)S(1)} %broadcast_clamp_fusion.6), kind=kCustom, calls=%fused_computation.1.clone | custom fusion | bytes 4202496 | tf_op jit(solution)/shard_map/jit(_take)/gather | solution.py:73
  131.9 9.1 %gather_fusion.2 = f32[2048,256]{1,0:T(8,128)S(1)} fusion(f32[5120,256]{1,0:T(8,128)} %bitcast.115, s32[2048]{0:T(1024)S(1)} %broadcast_clamp_fusion.5), kind=kCustom, calls=%fused_computation.2.clone | custom fusion | bytes 4202496 | tf_op jit(solution)/shard_map/jit(_take)/gather | solution.py:73
  142.9 9.1 %gather_fusion.3 = f32[2048,256]{1,0:T(8,128)S(1)} fusion(f32[5120,256]{1,0:T(8,128)} %bitcast.116, s32[2048]{0:T(1024)S(1)} %broadcast_clamp_fusion.4), kind=kCustom, calls=%fused_computation.3.clone | custom fusion | bytes 4202496 | tf_op jit(solution)/shard_map/jit(_take)/gather | solution.py:73
  153.9 9.1 %gather_fusion.4 = f32[2048,256]{1,0:T(8,128)S(1)} fusion(f32[5120,256]{1,0:T(8,128)} %bitcast.117, s32[2048]{0:T(1024)S(1)} %broadcast_clamp_fusion.3), kind=kCustom, calls=%fused_computation.4.clone | custom fusion | bytes 4202496 | tf_op jit(solution)/shard_map/jit(_take)/gather | solution.py:73
  164.9 9.1 %gather_fusion.5 = f32[2048,256]{1,0:T(8,128)S(1)} fusion(f32[5120,256]{1,0:T(8,128)} %bitcast.118, s32[2048]{0:T(1024)S(1)} %broadcast_clamp_fusion.2), kind=kCustom, calls=%fused_computation.5.clone | custom fusion | bytes 4202496 | tf_op jit(solution)/shard_map/jit(_take)/gather | solution.py:73
  175.9 9.1 %gather_fusion.6 = f32[2048,256]{1,0:T(8,128)S(1)} fusion(f32[5120,256]{1,0:T(8,128)} %bitcast.119, s32[2048]{0:T(1024)S(1)} %broadcast_clamp_fusion.1), kind=kCustom, calls=%fused_computation.6.clone | custom fusion | bytes 4202496 | tf_op jit(solution)/shard_map/jit(_take)/gather | solution.py:73
  186.9 9.1 %gather_fusion.7 = f32[2048,256]{1,0:T(8,128)S(1)} fusion(f32[5120,256]{1,0:T(8,128)} %bitcast.120, s32[2048]{0:T(1024)S(1)} %broadcast_clamp_fusion), kind=kCustom, calls=%fused_computation.7.clone | custom fusion | bytes 4202496 | tf_op jit(solution)/shard_map/jit(_take)/gather | solution.py:73
  197.9 9.7 %fusion = f32[4,512,256]{1,2,0:T(8,128)} fusion(f32[4,512,256]{1,2,0:T(8,128)} %copy.51, f32[4,512,256]{1,2,0:T(8,128)} %copy.50, f32[4,512,256]{1,2,0:T(8,128)} %copy.49, f32[4,512,256]{1,2,0:T(8,128)} %copy.48, f32[4,512,256]{1,2,0:T(8,128)} %copy.47, f32[4,512,256]{1,2,0:T(8,128)} %copy.46, f32[4,512,256]{1,2,0:T(8,128)} %copy.45, ...), kind=kLoop, calls=%fused_computation.10 | loop fusion | flops 12058624 | bytes 18956288 | tf_op jit(solution)/shard_map/add | solution.py:73
  211.5 3.2 copy.53
  214.7 11.6 %all-to-all-start = ((f32[64,8,2,512]{3,1,2,0:T(8,128)}), f32[64,8,2,512]{3,1,2,0:T(8,128)S(1)}, u32[]{:S(2)}, u32[]{:S(2)}) async-start(f32[64,8,2,512]{3,1,2,0:T(8,128)} %copy.53), calls=%async_computation | async-start | bytes 4194304 | tf_op jit(solution)/shard_map/all_to_all | solution.py:115
  226.8 49.0 %all-to-all-done = f32[64,8,2,512]{3,1,2,0:T(8,128)S(1)} async-done(((f32[64,8,2,512]{3,1,2,0:T(8,128)}), f32[64,8,2,512]{3,1,2,0:T(8,128)S(1)}, u32[]{:S(2)}, u32[]{:S(2)}) %all-to-all-start) | async-done | bytes 2097184 | tf_op jit(solution)/shard_map/all_to_all | solution.py:115
  284.6 3.0 fusion.26
  290.3 3.7 %fusion.10 = f32[8,256,128]{1,2,0:T(8,128)} fusion(f32[8,128,256]{2,1,0:T(8,128)S(1)} %fusion.26, f32[8,128,256]{1,2,0:T(8,128)S(1)} %fusion.7, f32[8,128,256]{1,2,0:T(8,128)S(1)} %fusion.8, f32[128,256]{0,1:T(8,128)S(1)} %get-tuple-element.33, f32[128,256]{0,1:T(8,128)S(1)} %get-tuple-element.34), kind=kOutput, calls=%fused_computation.31 | convolution fusion | flops 807534592 | bytes 4456448 | tf_op jit(solution)/shard_map/rbn,cn->rbc/dot_general | solution.py:62
  299.0 3.7 %fusion.12 = f32[8,256,128]{1,2,0:T(8,128)} fusion(f32[8,128,256]{2,1,0:T(8,128)S(1)} %fusion.30, f32[8,128,256]{1,2,0:T(8,128)S(1)} %fusion.7, f32[8,128,256]{1,2,0:T(8,128)S(1)} %fusion.8, f32[128,256]{0,1:T(8,128)S(1)} %get-tuple-element.33, f32[128,256]{0,1:T(8,128)S(1)} %get-tuple-element.34), kind=kOutput, calls=%fused_computation.34 | convolution fusion | flops 807534592 | bytes 4456448 | tf_op jit(solution)/shard_map/rbn,cn->rbc/dot_general | solution.py:59
  308.0 14.0 %psum.28 = f32[]{:T(128)} all-reduce(f32[]{:T(128)} %multiply_reduce_fusion), channel_id=1, replica_groups=mesh['rng'=8,'az_0'=8,'az_1'=4,'az_2'=2] {'rng'}, use_global_device_ids=true, to_apply=%region_1.3 | all-reduce | flops 1 | bytes 8 | tf_op jit(solution)/shard_map/psum | solution.py:26
  322.0 13.7 %psum.29 = f32[]{:T(128)} all-reduce(f32[]{:T(128)} %psum.28), channel_id=1, replica_groups=mesh['rng'=8,'az_0'=8,'az_1'=4,'az_2'=2] {'az_0'}, use_global_device_ids=true, to_apply=%region_2.4 | all-reduce | flops 1 | bytes 8 | tf_op jit(solution)/shard_map/psum | solution.py:26
  335.7 8.1 %psum.30 = f32[]{:T(128)} all-reduce(f32[]{:T(128)} %psum.29), channel_id=1, replica_groups=mesh['rng'=8,'az_0'=8,'az_1'=4,'az_2'=2] {'az_1'}, use_global_device_ids=true, to_apply=%region_3.5 | all-reduce | flops 1 | bytes 8 | tf_op jit(solution)/shard_map/psum | solution.py:26
  343.8 12.9 %psum.31 = f32[]{:T(128)} all-reduce(f32[]{:T(128)} %psum.30), channel_id=1, replica_groups=mesh['rng'=8,'az_0'=8,'az_1'=4,'az_2'=2] {'az_2'}, use_global_device_ids=true, to_apply=%region_4.6 | all-reduce | flops 1 | bytes 8 | tf_op jit(solution)/shard_map/psum | solution.py:26
  357.5 2.9 copy.65
  (62 shorter events, 47.8 us)
Async XLA Ops:
  8.6 4.0 %copy-start.3 = (s32[4,4]{1,0:T(4,128)S(1)}, s32[4,4]{1,0:T(4,128)}, u32[]{:S(2)}) copy-start(s32[4,4]{1,0:T(4,128)} %param.7) | copy-start | bytes 196
  8.6 4.1 %copy-start.2 = (s32[4,512]{1,0:T(4,128)S(1)}, s32[4,512]{1,0:T(4,128)}, u32[]{:S(2)}) copy-start(s32[4,512]{1,0:T(4,128)} %param.8) | copy-start | bytes 24580
  8.7 4.4 %copy-start.1 = (f32[8,4,512]{2,1,0:T(4,128)S(1)}, f32[8,4,512]{2,1,0:T(4,128)}, u32[]{:S(2)}) copy-start(f32[8,4,512]{2,1,0:T(4,128)} %param.9) | copy-start | bytes 196612
  8.7 97.0 %collective-permute-start = (f32[4,512,256]{2,1,0:T(8,128)S(1)}, f32[4,512,256]{2,1,0:T(8,128)}, u32[]{:S(2)}, u32[]{:S(2)}) collective-permute-start(f32[4,512,256]{2,1,0:T(8,128)S(1)} %reshape.100), channel_id=1, source_target_pairs={{64,0},{128,64},{192,128},{256,192},{320,256},{384,320},{448,384},... | collective-permute-start | bytes 6291464 | tf_op jit(solution)/shard_map/ppermute | solution.py:21
  11.1 94.6 %collective-permute-start.1 = (f32[4,256,256]{2,1,0:T(8,128)}, f32[4,256,256]{2,1,0:T(8,128)S(1)}, u32[]{:S(2)}, u32[]{:S(2)}) collective-permute-start(f32[4,256,256]{2,1,0:T(8,128)} %slice.60), channel_id=1, source_target_pairs={{128,0},{192,64},{256,128},{320,192},{384,256},{448,320},{129,1},{... | collective-permute-start | bytes 3145736 | tf_op jit(solution)/shard_map/ppermute | solution.py:21
  214.7 61.1 %all-to-all-start = ((f32[64,8,2,512]{3,1,2,0:T(8,128)}), f32[64,8,2,512]{3,1,2,0:T(8,128)S(1)}, u32[]{:S(2)}, u32[]{:S(2)}) async-start(f32[64,8,2,512]{3,1,2,0:T(8,128)} %copy.53), calls=%async_computation | async-start | bytes 4194304 | tf_op jit(solution)/shard_map/all_to_all | solution.py:115
  304.3 2.5 copy-start
where the time goes:
time: 365 us; the launch traced here: 361 us
  waiting for transfers between devices  142 us (39%)
  local copies, waits for them, and re-layouts  117 us (32%)
  blocking collectives  48.7 us (13%)
  matrix products  21.6 us (6%)
  other arithmetic  16 us (4%)
  starting transfers between devices  14.5 us (4%)
    ppermute x2, waiting for transfers between devices, from_behind(): return lax.ppermute(shard, axis, pairs)  92.6 us
    gather x16, local copies, waits for them, and re-layouts, apply_taps(): jnp.take(flat, flat_rows + tap_index, axis=0)  87.8 us
    all_to_all x1, waiting for transfers between devices, body(): lax.all_to_all(ordered, AZ, split_axis=0, concat_axis=3, tiled=True)  49 us
    psum x4, blocking collectives, by_axis(): shard = lax.psum(shard, axis)  48.7 us
    all_to_all x1, starting transfers between devices, body(): lax.all_to_all(ordered, AZ, split_axis=0, concat_axis=3, tiled=True)  11.6 us
    add x1, other arithmetic, apply_taps(): result + weights[tap_index][:, :, None] * jnp.take(flat, flat_rows + tap_...  9.72 us
  transfers between devices with their start and end apart: 3, of which 2 were waited for; matrix products, arithmetic and copies ran while one was open for 1% of the time, Pallas kernels for 0%

commit v1 on v0

v1 whole, which is shorter than its diff:
```python
import math

import jax
import jax.numpy as jnp
import numpy as np
from jax import lax
from jax.experimental import pallas as pl
from jax.experimental.pallas import tpu as pltpu
from jax.sharding import Mesh
from jax.sharding import PartitionSpec as P

BLOCK = 128
GW = 128
TAPS = 8
HEAD = 136
WIN = 144
AZ = ("az_0", "az_1", "az_2")
RNG_AZ = ("rng", "az_0", "az_1", "az_2")
CHUNKS = ((0,), (1, 3), (2,))
FULL = 63 << 20
ROOM = pltpu.CompilerParams(vmem_limit_bytes=12 << 20)
VMEM = pl.BlockSpec(memory_space=pltpu.VMEM)
SMEM = pl.BlockSpec(memory_space=pltpu.SMEM)


def halves(x):
    high = x.astype(jnp.bfloat16)
    return high, (x - high.astype(jnp.float32)).astype(jnp.bfloat16)


def product(a, b, contract):
    a_high, a_low = a
    b_high, b_low = b

    def times(x, y):
        return lax.dot_general(x, y, (contract, ((), ())), preferred_element_type=jnp.float32)

    return times(a_high, b_high) + times(a_high, b_low) + times(a_low, b_high)


def split_table(table):
    high = table.astype(jnp.bfloat16)
    low = (table - high.astype(np.float64)).astype(jnp.bfloat16)
    return high, low


def first_table(upper):
    a = 2 * np.arange(64) + upper
    ang = (a[:, None] * np.arange(128)[None, :] % 128) * (2 * math.pi / 128)
    cos, sin = np.cos(ang), np.sin(ang)
    return split_table(np.block([[cos, sin], [-sin, cos]]))


def turn_table(half):
    ang = (np.arange(128)[:, None] + 128 * half) * np.arange(128)[None, :] * (2 * math.pi / 32768)
    return np.stack([np.cos(ang), np.sin(ang)]).astype(np.float32)


def second_table(half):
    m = np.arange(128) + 128 * half
    ang = (np.arange(256)[:, None] * m[None] % 256) * (2 * math.pi / 256)
    cos, sin = np.cos(ang) / 32768, np.sin(ang) / 32768
    real = np.concatenate([cos, -sin], axis=1)
    imag = np.concatenate([sin, cos], axis=1)
    return split_table(np.stack([real, imag], axis=1).reshape(512, 256))


def regroup_kernel(x_ref, *out_refs):
    for index, chunk in enumerate(CHUNKS):
        head, rest = out_refs[2 * index], out_refs[2 * index + 1]
        for at, g in enumerate(chunk):
            for c in range(2):
                lanes = pl.ds(128 * c, 128)
                head[at, :, lanes] = x_ref[pl.ds(2 * g + c, HEAD, stride=8), :]
                rest[at, :, lanes] = x_ref[pl.ds(8 * HEAD + 2 * g + c, 512 - HEAD, stride=8), :]


def regroup(flat):
    shapes = []
    for chunk in CHUNKS:
        shapes.append(jax.ShapeDtypeStruct((len(chunk), HEAD, 256), jnp.float32))
        shapes.append(jax.ShapeDtypeStruct((len(chunk), 512 - HEAD, 256), jnp.float32))
    return pl.pallas_call(
        regroup_kernel,
        out_shape=shapes,
        name="regroup",
        compiler_params=ROOM,
    )(flat)


def remap_kernel(src_ref, off_ref, w_ref, a0, b0, a1, b1, a2, before_ref, out_ref, energy_ref, ext):
    count = a0.shape[0]
    energy = before_ref[...]
    ext[1024 + HEAD :, :] = jnp.zeros((ext.shape[0] - 1024 - HEAD, 256), jnp.float32)
    rows = lax.broadcasted_iota(jnp.int32, (WIN, BLOCK), 0)
    for at in range(count):
        ext[0:HEAD, :] = a0[at]
        ext[HEAD:512, :] = b0[at]
        ext[512 : 512 + HEAD, :] = a1[at]
        ext[512 + HEAD : 1024, :] = b1[at]
        ext[1024 : 1024 + HEAD, :] = a2[at]
        for b in range(4):
            start = pl.multiple_of(src_ref[at, b] * BLOCK, BLOCK)
            source = ext[pl.ds(start, WIN), :]
            here = pl.ds(b * BLOCK, BLOCK)
            tap_at = rows - off_ref[at, :, here]
            weights = jnp.zeros((WIN, BLOCK), jnp.float32)
            for t in range(TAPS):
                weights = jnp.where(tap_at == t, w_ref[at, pl.ds(t, 1), here], weights)
            w_high, w_low = halves(weights)
            s_high, s_low = halves(source)
            result = lax.dot_general(
                jnp.concatenate([w_high, w_high, w_low], axis=0),
                jnp.concatenate([s_high, s_low, s_high], axis=0),
                (((0,), (0,)), ((), ())),
                preferred_element_type=jnp.float32,
            )
            for c in range(2):
                part = result[:, 128 * c : 128 * c + 128].reshape(16, 8, 128)
                out_ref[pl.ds(16 * b, 16), at, c] = part
                energy = energy + jnp.sum(part * part, axis=0)
    energy_ref[...] = energy


def remap(src, off, weights, parts, before):
    count = off.shape[0]
    return pl.pallas_call(
        remap_kernel,
        out_shape=[
            jax.ShapeDtypeStruct((64, count, 2, 8, 128), jnp.float32),
            jax.ShapeDtypeStruct((8, 128), jnp.float32),
        ],
        in_specs=[SMEM] + [VMEM] * 8,
        out_specs=[VMEM, VMEM],
        scratch_shapes=[pltpu.VMEM((1024 + WIN, 256), jnp.float32)],
        compiler_params=ROOM,
    )(src, off, weights, *parts, before)


def pack_kernel(x_ref, energy_ref, out_ref):
    total = jnp.full((1, 128), jnp.sum(energy_ref[...]), jnp.float32)
    for a in range(64):
        out_ref[pl.ds(17 * a, 8), :] = x_ref[a, 0, 0]
        out_ref[pl.ds(17 * a + 8, 8), :] = x_ref[a, 0, 1]
        out_ref[pl.ds(17 * a + 16, 1), :] = total


def pack(x, energy):
    return pl.pallas_call(
        pack_kernel,
        out_shape=jax.ShapeDtypeStruct((64 * 17, 128), jnp.float32),
        in_specs=[VMEM, VMEM],
        out_specs=VMEM,
        name="pack",
        compiler_params=ROOM,
    )(x, energy)


def columns(ref, at, stride, rows):
    lanes = []
    for r in rows:
        parts = [ref[pl.ds(16 * at + 8 * c + r, 64, stride=stride), :] for c in range(2)]
        lanes.append(jnp.concatenate(parts, axis=0))
    return halves(jnp.concatenate(lanes, axis=1))


def turned(step, cos, sin):
    lanes = []
    for r in range(step.shape[0] // 128):
        real, imag = step[128 * r : 128 * r + 128, :128], step[128 * r : 128 * r + 128, 128:]
        both = [real * cos - imag * sin, real * sin + imag * cos]
        lanes.append(jnp.concatenate(both, axis=0))
    return halves(jnp.concatenate(lanes, axis=1))


ROWS = ((0,), (0,))
INNER = ((1,), (0,))


def early_kernel(x0, x13, f0h, f0l, f1h, f1l, turn, mh, ml, step_ref, part_ref):
    low = (f0h[...], f0l[...])
    high = (f1h[...], f1l[...])
    step_ref[...] = product(columns(x0, 0, 16, range(8)), low, ROWS)
    for i in range(4):
        rows = (2 * i, 2 * i + 1)
        step = product(columns(x13, 0, 32, rows), low, ROWS)
        step = step + product(columns(x13, 1, 32, rows), high, ROWS)
        data = turned(step, turn[0], turn[1])
        part_ref[:, pl.ds(256 * i, 256)] = product((mh[...], ml[...]), data, INNER)


def early(x0, x13, tables):
    return pl.pallas_call(
        early_kernel,
        out_shape=[
            jax.ShapeDtypeStruct((1024, 256), jnp.float32),
            jax.ShapeDtypeStruct((512, 1024), jnp.float32),
        ],
        in_specs=[VMEM] * 9,
        out_specs=[VMEM, VMEM],
        name="early",
        compiler_params=ROOM,
    )(x0, x13, *tables)


def finish_kernel(x2, step_ref, part_ref, f1h, f1l, turn, mh, ml, out_ref):
    i = pl.program_id(0)
    energy = jnp.sum(x2[pl.ds(16, 64, stride=17), :], axis=0, keepdims=True)
    scale = lax.rsqrt(energy * (1.0 / (32768.0 * 134217728.0)) + 1e-06)
    step = step_ref[...] + product(
        columns(x2, 0, 17, (2 * i, 2 * i + 1)), (f1h[...], f1l[...]), ROWS
    )
    data = turned(step, turn[0], turn[1])
    result = part_ref[...] + product((mh[...], ml[...]), data, INNER)
    for at in range(2):
        out_ref[at] = result[:, 128 * at : 128 * at + 128] * scale


def finish(x2, step, part, tables):
    def whole(shape):
        return pl.BlockSpec(shape, lambda i: (0,) * len(shape))

    return pl.pallas_call(
        finish_kernel,
        out_shape=jax.ShapeDtypeStruct((8, 512, 128), jnp.float32),
        grid=(4,),
        in_specs=[
            whole((1088, 128)),
            pl.BlockSpec((256, 256), lambda i: (i, 0)),
            pl.BlockSpec((512, 256), lambda i: (0, i)),
        ]
        + [whole(t.shape) for t in tables],
        out_specs=pl.BlockSpec((2, 512, 128), lambda i: (i, 0, 0)),
        name="finish",
        compiler_params=pltpu.CompilerParams(vmem_limit_bytes=FULL),
    )(x2, step, part, *tables)


def steps(spectrum, src_block, offsets, tap_weights):
    position = lax.axis_index("rng")
    size = lax.axis_size("rng")
    down = [(i, i - 1) for i in range(1, size)]
    flat = spectrum.reshape(512, 2, 4, GW).transpose(0, 2, 1, 3).reshape(4096, GW)
    local = regroup(flat)
    src = jnp.clip(src_block - 4 * position, 0, 8)
    off = offsets.reshape(4, 1, 512)
    weights = tap_weights.transpose(1, 0, 2)

    def pull(x):
        return lax.ppermute(x, "rng", down)

    def swap(x):
        return lax.all_to_all(x, AZ, split_axis=0, concat_axis=0, tiled=True)

    energy = jnp.zeros((8, 128), jnp.float32)
    moved = []
    for i, chunk in enumerate(CHUNKS):
        near, far = local[2 * i], local[2 * i + 1]
        near_up = pull(near)
        far_up = pull(far)
        near_up_up = pull(near_up)

        def of_chunk(x):
            return jnp.concatenate([x[g : g + 1] for g in chunk], axis=0)

        out, energy = remap(
            of_chunk(src),
            of_chunk(off),
            of_chunk(weights),
            (near, far, near_up, far_up, near_up_up),
            energy,
        )
        moved.append(out)
    got0 = swap(moved[0]).reshape(1024, 128)
    got1 = swap(moved[1]).reshape(2048, 128)
    energy = lax.psum(energy, "rng")
    packed = pack(moved[2], energy).reshape(64, 1, 17 * 128)
    got2 = swap(packed).reshape(1088, 128)
    f0, f1 = first_table(0), first_table(1)
    step, part = early(got0, got1, (*f0, *f1, turn_table(1), *second_table(1)))
    out = finish(got2, step, part, (*f1, turn_table(0), *second_table(0)))
    return out.reshape(8, 256, 2, 128).transpose(0, 2, 1, 3).reshape(8, 2, 32768)


def solution(mesh):
    torus = Mesh(mesh.devices.reshape(mesh.shape["rng"], 8, 4, 2), RNG_AZ)
    placed = (P("rng", None, AZ), P(AZ, "rng"), P(AZ, "rng"), P(None, AZ, "rng"))
    return jax.shard_map(
        steps, mesh=torus, in_specs=placed, out_specs=P(RNG_AZ, None, None), check_vma=False
    )
```

time: 365 us -> 169 us (0.46)
  local copies, waits for them, and re-layouts: 117 us -> 4.86 us
  waiting for transfers between devices: 142 us -> 77.9 us
  starting transfers between devices: 14.5 us -> 53.7 us
  blocking collectives: 48.7 us -> 15.4 us
  matrix products: 21.6 us -> 0 us
  other arithmetic: 16 us -> 0.02 us
  Pallas kernels: 0 us -> 15.9 us
    gather x16 -> x0, local copies, waits for them, and re-layouts: 87.8 us -> none  [apply_taps(): jnp.take(flat, flat_rows + tap_index, axis=0)]
    all_to_all x1 -> x3, waiting for transfers between devices: 49 us -> 11.9 us  [swap(): return lax.all_to_all(x, AZ, split_axis=0, concat_axis=0, tiled=True)]
    psum x4 -> x1, blocking collectives: 48.7 us -> 15.4 us  [steps(): energy = lax.psum(energy, 'rng')]
    all_to_all x1 -> x3, starting transfers between devices: 11.6 us -> 42 us  [swap(): return lax.all_to_all(x, AZ, split_axis=0, concat_axis=0, tiled=True)]
    ppermute x2 -> x9, waiting for transfers between devices: 92.6 us -> 65.9 us  [pull(): return lax.ppermute(x, 'rng', down)]
    dot_general x8 -> x0, matrix products: 21.6 us -> none  [the longest x1 3.7 us: inverse_rows(): jnp.einsum('rbn,cn->rbc', turned_imag, second_sin, precision=highest)]
    pallas_call x0 -> x7, Pallas kernels: none -> 15.9 us  [the longest x1 6.18 us: finish(): pl.pallas_call(finish_kernel, out_shape=jax.ShapeDtypeStruct((8, 512, 128...]
    reshape x4 -> x0, local copies, waits for them, and re-layouts: 11.2 us -> none  [the longest x2 5.03 us: body(): ordered = remapped.reshape(groups, rows_dev, 2, GW).transpose(1, 2, 0, 3)...]
  transfers between devices with their start and end apart: 3 -> 12, of which waited for: 2 -> 7; matrix products, arithmetic and copies ran while one was open for 1% -> 0% of each run, Pallas kernels for 0% -> 4%
where the time goes in v1:
time: 169 us; the launch traced here: 168 us
  waiting for transfers between devices  77.9 us (46%)
  starting transfers between devices  53.7 us (32%)
  Pallas kernels  15.9 us (9%)
  blocking collectives  15.4 us (9%)
  local copies, waits for them, and re-layouts  4.86 us (3%)
    ppermute x9, waiting for transfers between devices, pull(): return lax.ppermute(x, 'rng', down)  65.9 us
    all_to_all x3, starting transfers between devices, swap(): return lax.all_to_all(x, AZ, split_axis=0, concat_axis=0, tiled=True)  42 us
    psum x1, blocking collectives, steps(): energy = lax.psum(energy, 'rng')  15.4 us
    all_to_all x3, waiting for transfers between devices, swap(): return lax.all_to_all(x, AZ, split_axis=0, concat_axis=0, tiled=True)  11.9 us
    ppermute x9, starting transfers between devices, pull(): return lax.ppermute(x, 'rng', down)  11.7 us
    pallas_call x1, Pallas kernels, finish(): pl.pallas_call(finish_kernel, out_shape=jax.ShapeDtypeStruct((8, 512, 128...  6.18 us
    pallas_call x3, Pallas kernels, remap(): pl.pallas_call(remap_kernel, out_shape=[jax.ShapeDtypeStruct((64, count,...  5.22 us
    unnamed x27, local copies, waits for them, and re-layouts  4.84 us
  transfers between devices with their start and end apart: 12, of which 7 were waited for; matrix products, arithmetic and copies ran while one was open for 0% of the time, Pallas kernels for 4%

profile of v1, /device:TPU:1, one launch (start us, length us, event | category | flops | bytes accessed | tf_op | source)
XLA Modules:
  0.0 168.2 jit_solution(865687880962719236)
XLA Ops:
  0.0 1.6 copy-done.1
  2.1 1.3 collective-permute-start.6
  3.4 1.3 collective-permute-start.7
  4.8 4.5 %collective-permute-done.6.a1 = f32[1,136,256]{2,1,0:T(8,128)S(1)} collective-permute-done((f32[1,136,256]{2,1,0:T(8,128)S(1)}, f32[1,136,256]{2,1,0:T(8,128)S(1)}, u32[]{:S(2)}, u32[]{:S(2)}) %collective-permute-start.6) | collective-permute-done | bytes 139296 | tf_op jit(solution)/shard_map/ppermute | solution.py:250
  9.3 1.3 collective-permute-start.8
  10.6 7.8 %collective-permute-done.8.a2 = f32[1,136,256]{2,1,0:T(8,128)S(1)} collective-permute-done((f32[1,136,256]{2,1,0:T(8,128)S(1)}, f32[1,136,256]{2,1,0:T(8,128)S(1)}, u32[]{:S(2)}, u32[]{:S(2)}) %collective-permute-start.8) | collective-permute-done | bytes 139296 | tf_op jit(solution)/shard_map/ppermute | solution.py:250
  18.4 1.8 %shard_map.136 = (f32[64,1,2,8,128]{4,3,2,1,0:T(8,128)}, f32[8,128]{1,0:T(8,128)S(1)}) custom-call(s32[1,4]{1,0:T(1,128)S(1)} %get-tuple-element.41.src_ref, s32[1,1,512]{2,1,0:T(1,128)S(1)} %get-tuple-element.37.off_ref, f32[1,8,512]{2,1,0:T(8,128)S(1)} %get-tuple-element.33.w_ref, f32[1,136,256]{2,1,0:T(8,128)S(1)} %get-tuple-element.23.a0, ...), custom_call_target="tpu_custom_call" | custom-call | tf_op jit(solution)/shard_map/pallas_call | solution.py:127
  20.3 14.4 %all-to-all-start.1 = ((f32[64,1,2,8,128]{4,3,2,1,0:T(8,128)}), f32[64,1,2,8,128]{4,3,2,1,0:T(8,128)S(1)}, u32[]{:S(2)}, u32[]{:S(2)}) async-start(f32[64,1,2,8,128]{4,3,2,1,0:T(8,128)} %get-tuple-element.29), calls=%async_computation.1 | async-start | bytes 1048576 | tf_op jit(solution)/shard_map/all_to_all | solution.py:253
  34.7 1.3 collective-permute-start.4
  36.0 1.3 collective-permute-start.3
  37.3 24.5 %collective-permute-done.3.a1 = f32[2,136,256]{2,1,0:T(8,128)S(1)} collective-permute-done((f32[2,136,256]{2,1,0:T(8,128)S(1)}, f32[2,136,256]{2,1,0:T(8,128)S(1)}, u32[]{:S(2)}, u32[]{:S(2)}) %collective-permute-start.3) | collective-permute-done | bytes 278560 | tf_op jit(solution)/shard_map/ppermute | solution.py:250
  63.1 8.7 %collective-permute-done.5.a2 = f32[2,136,256]{2,1,0:T(8,128)S(1)} collective-permute-done((f32[2,136,256]{2,1,0:T(8,128)S(1)}, f32[2,136,256]{2,1,0:T(8,128)S(1)}, u32[]{:S(2)}, u32[]{:S(2)}) %collective-permute-start.5) | collective-permute-done | bytes 278560 | tf_op jit(solution)/shard_map/ppermute | solution.py:250
  71.8 2.4 %shard_map.137 = (f32[64,2,2,8,128]{4,3,2,1,0:T(8,128)}, f32[8,128]{1,0:T(8,128)S(1)}) custom-call(s32[2,4]{1,0:T(2,128)S(1)} %pad_add_fusion.1.src_ref, s32[2,1,512]{2,1,0:T(1,128)S(1)} %pad_add_fusion.off_ref, f32[2,8,512]{2,1,0:T(8,128)S(1)} %pad_maximum_fusion.w_ref, f32[2,136,256]{2,1,0:T(8,128)S(1)} %get-tuple-element.21.a0, ...), custom_call_target="tpu_custom_call" | custom-call | tf_op jit(solution)/shard_map/pallas_call | solution.py:127
  74.1 11.6 %all-to-all-start.2 = ((f32[64,2,2,8,128]{4,3,2,1,0:T(8,128)}), f32[64,2,2,8,128]{4,3,2,1,0:T(8,128)S(1)}, u32[]{:S(2)}, u32[]{:S(2)}) async-start(f32[64,2,2,8,128]{4,3,2,1,0:T(8,128)} %get-tuple-element.30), calls=%async_computation.2 | async-start | bytes 2097152 | tf_op jit(solution)/shard_map/all_to_all | solution.py:253
  85.8 1.4 collective-permute-start.1
  87.2 1.3 collective-permute-start
  88.5 14.4 %collective-permute-done.a1 = f32[1,136,256]{2,1,0:T(8,128)S(1)} collective-permute-done((f32[1,136,256]{2,1,0:T(8,128)S(1)}, f32[1,136,256]{2,1,0:T(8,128)S(1)}, u32[]{:S(2)}, u32[]{:S(2)}) %collective-permute-start) | collective-permute-done | bytes 139296 | tf_op jit(solution)/shard_map/ppermute | solution.py:250
  104.3 6.0 %collective-permute-done.2.a2 = f32[1,136,256]{2,1,0:T(8,128)S(1)} collective-permute-done((f32[1,136,256]{2,1,0:T(8,128)S(1)}, f32[1,136,256]{2,1,0:T(8,128)S(1)}, u32[]{:S(2)}, u32[]{:S(2)}) %collective-permute-start.2) | collective-permute-done | bytes 139296 | tf_op jit(solution)/shard_map/ppermute | solution.py:250
  111.3 15.4 %psum.7.energy_ref = f32[8,128]{1,0:T(8,128)S(1)} all-reduce(f32[8,128]{1,0:T(8,128)S(1)} %get-tuple-element.28), channel_id=1, replica_groups=mesh['rng'=8,'az_0'=8,'az_1'=4,'az_2'=2] {'rng'}, use_global_device_ids=true, to_apply=%region_0.1 | all-reduce | flops 1024 | bytes 8192 | tf_op jit(solution)/shard_map/psum | solution.py:276
  127.7 16.0 %all-to-all-start = ((f32[64,1,2176]{2,1,0:T(1,128)}), f32[64,1,2176]{2,1,0:T(1,128)}, u32[]{:S(2)}, u32[]{:S(2)}) async-start(f32[64,1,2176]{2,1,0:T(1,128)} %bitcast.8), calls=%async_computation | async-start | bytes 1114112 | tf_op jit(solution)/shard_map/all_to_all | solution.py:253
  144.6 3.1 %early.1 = (f32[1024,256]{1,0:T(8,128)S(1)}, f32[512,1024]{1,0:T(8,128)S(1)}) custom-call(f32[1024,128]{1,0:T(8,128)S(1)} %bitcast.26, f32[2048,128]{1,0:T(8,128)S(1)} %bitcast.25, bf16[128,256]{1,0:T(8,128)(2,1)S(1)} %copy-done.9, bf16[128,256]{1,0:T(8,128)(2,1)S(1)} %copy-done.8, bf16[128,256]{1,0:T(8,128)(2,1)S(1)} %copy-done.4, ...), custom_call_target="tpu_custom_call" | custom-call | tf_op jit(solution)/shard_map/early/pallas_call | solution.py:193
  147.7 1.3 copy-done
  150.1 11.9 %all-to-all-done = f32[64,1,2176]{2,1,0:T(1,128)} async-done(((f32[64,1,2176]{2,1,0:T(1,128)}), f32[64,1,2176]{2,1,0:T(1,128)}, u32[]{:S(2)}, u32[]{:S(2)}) %all-to-all-start) | async-done | bytes 557088 | tf_op jit(solution)/shard_map/all_to_all | solution.py:253
  162.0 6.2 %finish.1 = f32[8,512,128]{2,1,0:T(8,128)} custom-call(f32[1088,128]{1,0:T(8,128)} %bitcast.9.x2, f32[1024,256]{1,0:T(8,128)} %copy-done.2, f32[512,1024]{1,0:T(8,128)} %copy-done, bf16[128,256]{1,0:T(8,128)(2,1)} %constant.36.clone.f1h, bf16[128,256]{1,0:T(8,128)(2,1)} %constant.37.clone.f1l, f32[2,128,128]{2,1,0:T(8,128)} %constant.41.clone.turn, ...), custom_call_target="tpu_custom_call" | custom-call | tf_op jit(solution)/shard_map/finish/pallas_call | solution.py:223
  (43 shorter events, 7.0 us)
Async XLA Ops:
  0.0 1.6 copy-start.1
  1.6 3.1 %copy-start.11 = (s32[4,512]{1,0:T(4,128)S(1)}, s32[4,512]{1,0:T(4,128)}, u32[]{:S(2)}) copy-start(s32[4,512]{1,0:T(4,128)} %param.16) | copy-start | bytes 24580
  1.6 3.1 %copy-start.10 = (f32[8,4,512]{2,1,0:T(4,128)S(1)}, f32[8,4,512]{2,1,0:T(4,128)}, u32[]{:S(2)}) copy-start(f32[8,4,512]{2,1,0:T(4,128)} %param.17) | copy-start | bytes 196612
  1.6 3.2 %copy-start.12 = (s32[4,4]{1,0:T(4,128)S(1)}, s32[4,4]{1,0:T(4,128)}, u32[]{:S(2)}) copy-start(s32[4,4]{1,0:T(4,128)} %param.15) | copy-start | bytes 196
  2.1 7.3 %collective-permute-start.6 = (f32[1,136,256]{2,1,0:T(8,128)S(1)}, f32[1,136,256]{2,1,0:T(8,128)S(1)}, u32[]{:S(2)}, u32[]{:S(2)}) collective-permute-start(f32[1,136,256]{2,1,0:T(8,128)S(1)} %get-tuple-element.23.a0), channel_id=1, source_target_pairs={{64,0},{128,64},{192,128},{256,192},{320,256},{384,320},{448,384},... | collective-permute-start | bytes 417800 | tf_op jit(solution)/shard_map/ppermute | solution.py:250
  3.4 15.1 %collective-permute-start.7 = (f32[1,376,256]{2,1,0:T(8,128)S(1)}, f32[1,376,256]{2,1,0:T(8,128)S(1)}, u32[]{:S(2)}, u32[]{:S(2)}) collective-permute-start(f32[1,376,256]{2,1,0:T(8,128)S(1)} %get-tuple-element.24.b0), channel_id=1, source_target_pairs={{64,0},{128,64},{192,128},{256,192},{320,256},{384,320},{448,384},... | collective-permute-start | bytes 1155080 | tf_op jit(solution)/shard_map/ppermute | solution.py:250
  9.3 9.1 %collective-permute-start.8 = (f32[1,136,256]{2,1,0:T(8,128)S(1)}, f32[1,136,256]{2,1,0:T(8,128)S(1)}, u32[]{:S(2)}, u32[]{:S(2)}) collective-permute-start(f32[1,136,256]{2,1,0:T(8,128)S(1)} %collective-permute-done.6.a1), channel_id=1, source_target_pairs={{64,0},{128,64},{192,128},{256,192},{320,256},{384,320},{448,384},... | collective-permute-start | bytes 417800 | tf_op jit(solution)/shard_map/ppermute | solution.py:250
  20.3 53.9 %all-to-all-start.1 = ((f32[64,1,2,8,128]{4,3,2,1,0:T(8,128)}), f32[64,1,2,8,128]{4,3,2,1,0:T(8,128)S(1)}, u32[]{:S(2)}, u32[]{:S(2)}) async-start(f32[64,1,2,8,128]{4,3,2,1,0:T(8,128)} %get-tuple-element.29), calls=%async_computation.1 | async-start | bytes 1048576 | tf_op jit(solution)/shard_map/all_to_all | solution.py:253
  34.7 37.1 %collective-permute-start.4 = (f32[2,376,256]{2,1,0:T(8,128)S(1)}, f32[2,376,256]{2,1,0:T(8,128)S(1)}, u32[]{:S(2)}, u32[]{:S(2)}) collective-permute-start(f32[2,376,256]{2,1,0:T(8,128)S(1)} %get-tuple-element.22.b0), channel_id=1, source_target_pairs={{64,0},{128,64},{192,128},{256,192},{320,256},{384,320},{448,384},... | collective-permute-start | bytes 2310152 | tf_op jit(solution)/shard_map/ppermute | solution.py:250
  36.0 25.8 %collective-permute-start.3 = (f32[2,136,256]{2,1,0:T(8,128)S(1)}, f32[2,136,256]{2,1,0:T(8,128)S(1)}, u32[]{:S(2)}, u32[]{:S(2)}) collective-permute-start(f32[2,136,256]{2,1,0:T(8,128)S(1)} %get-tuple-element.21.a0), channel_id=1, source_target_pairs={{64,0},{128,64},{192,128},{256,192},{320,256},{384,320},{448,384},... | collective-permute-start | bytes 835592 | tf_op jit(solution)/shard_map/ppermute | solution.py:250
  61.8 10.0 %collective-permute-start.5 = (f32[2,136,256]{2,1,0:T(8,128)S(1)}, f32[2,136,256]{2,1,0:T(8,128)S(1)}, u32[]{:S(2)}, u32[]{:S(2)}) collective-permute-start(f32[2,136,256]{2,1,0:T(8,128)S(1)} %collective-permute-done.3.a1), channel_id=1, source_target_pairs={{64,0},{128,64},{192,128},{256,192},{320,256},{384,320},{448,384},... | collective-permute-start | bytes 835592 | tf_op jit(solution)/shard_map/ppermute | solution.py:250
  74.1 53.6 %all-to-all-start.2 = ((f32[64,2,2,8,128]{4,3,2,1,0:T(8,128)}), f32[64,2,2,8,128]{4,3,2,1,0:T(8,128)S(1)}, u32[]{:S(2)}, u32[]{:S(2)}) async-start(f32[64,2,2,8,128]{4,3,2,1,0:T(8,128)} %get-tuple-element.30), calls=%async_computation.2 | async-start | bytes 2097152 | tf_op jit(solution)/shard_map/all_to_all | solution.py:253
  85.7 58.0 %copy-start.3 = (bf16[128,256]{1,0:T(8,128)(2,1)S(1)}, bf16[128,256]{1,0:T(8,128)(2,1)}, u32[]{:S(2)}) copy-start(bf16[128,256]{1,0:T(8,128)(2,1)} %constant.37.clone.f1l) | copy-start | bytes 196612
  85.7 58.0 %copy-start.4 = (bf16[128,256]{1,0:T(8,128)(2,1)S(1)}, bf16[128,256]{1,0:T(8,128)(2,1)}, u32[]{:S(2)}) copy-start(bf16[128,256]{1,0:T(8,128)(2,1)} %constant.36.clone.f1h) | copy-start | bytes 196612
  85.7 58.0 %copy-start.5 = (bf16[512,256]{1,0:T(8,128)(2,1)S(1)}, bf16[512,256]{1,0:T(8,128)(2,1)}, u32[]{:S(2)}) copy-start(bf16[512,256]{1,0:T(8,128)(2,1)} %constant.40.clone.ml) | copy-start | bytes 786436
  85.8 58.0 %copy-start.6 = (bf16[512,256]{1,0:T(8,128)(2,1)S(1)}, bf16[512,256]{1,0:T(8,128)(2,1)}, u32[]{:S(2)}) copy-start(bf16[512,256]{1,0:T(8,128)(2,1)} %constant.39.clone.mh) | copy-start | bytes 786436
  85.8 58.0 %copy-start.7 = (f32[2,128,128]{2,1,0:T(8,128)S(1)}, f32[2,128,128]{2,1,0:T(8,128)}, u32[]{:S(2)}) copy-start(f32[2,128,128]{2,1,0:T(8,128)} %constant.38.clone.turn) | copy-start | bytes 393220
  85.8 58.0 %copy-start.8 = (bf16[128,256]{1,0:T(8,128)(2,1)S(1)}, bf16[128,256]{1,0:T(8,128)(2,1)}, u32[]{:S(2)}) copy-start(bf16[128,256]{1,0:T(8,128)(2,1)} %constant.35.clone.f0l) | copy-start | bytes 196612
  85.8 24.5 %collective-permute-start.1 = (f32[1,376,256]{2,1,0:T(8,128)S(1)}, f32[1,376,256]{2,1,0:T(8,128)S(1)}, u32[]{:S(2)}, u32[]{:S(2)}) collective-permute-start(f32[1,376,256]{2,1,0:T(8,128)S(1)} %get-tuple-element.20.b0), channel_id=1, source_target_pairs={{64,0},{128,64},{192,128},{256,192},{320,256},{384,320},{448,384},... | collective-permute-start | bytes 1155080 | tf_op jit(solution)/shard_map/ppermute | solution.py:250
  87.2 15.7 %collective-permute-start = (f32[1,136,256]{2,1,0:T(8,128)S(1)}, f32[1,136,256]{2,1,0:T(8,128)S(1)}, u32[]{:S(2)}, u32[]{:S(2)}) collective-permute-start(f32[1,136,256]{2,1,0:T(8,128)S(1)} %get-tuple-element.19.a0), channel_id=1, source_target_pairs={{64,0},{128,64},{192,128},{256,192},{320,256},{384,320},{448,384},... | collective-permute-start | bytes 417800 | tf_op jit(solution)/shard_map/ppermute | solution.py:250
  103.0 7.3 %collective-permute-start.2 = (f32[1,136,256]{2,1,0:T(8,128)S(1)}, f32[1,136,256]{2,1,0:T(8,128)S(1)}, u32[]{:S(2)}, u32[]{:S(2)}) collective-permute-start(f32[1,136,256]{2,1,0:T(8,128)S(1)} %collective-permute-done.a1), channel_id=1, source_target_pairs={{64,0},{128,64},{192,128},{256,192},{320,256},{384,320},{448,384},... | collective-permute-start | bytes 417800 | tf_op jit(solution)/shard_map/ppermute | solution.py:250
  127.7 34.3 %all-to-all-start = ((f32[64,1,2176]{2,1,0:T(1,128)}), f32[64,1,2176]{2,1,0:T(1,128)}, u32[]{:S(2)}, u32[]{:S(2)}) async-start(f32[64,1,2176]{2,1,0:T(1,128)} %bitcast.8), calls=%async_computation | async-start | bytes 1114112 | tf_op jit(solution)/shard_map/all_to_all | solution.py:253
  147.7 1.4 copy-start
  149.1 1.0 copy-start.2
  (1 other events, 0.8 us)

commit v2 on v1

v2 whole, which is shorter than its diff:
```python
import math

import jax
import jax.numpy as jnp
import numpy as np
from jax import lax
from jax.experimental import pallas as pl
from jax.experimental.pallas import tpu as pltpu
from jax.sharding import Mesh
from jax.sharding import PartitionSpec as P

BLOCK = 128
GW = 128
TAPS = 8
HEAD = 136
WIN = 144
AZ = ("az_0", "az_1", "az_2")
RNG_AZ = ("rng", "az_0", "az_1", "az_2")
CHUNKS = (((3, 0), (3, 1)), ((1, 0), (1, 1), (0, 0)), ((0, 1), (2, 0), (2, 1)))
FULL = 63 << 20
ROOM = pltpu.CompilerParams(vmem_limit_bytes=12 << 20)
VMEM = pl.BlockSpec(memory_space=pltpu.VMEM)
ANY = pl.BlockSpec(memory_space=pl.ANY)
SMEM = pl.BlockSpec(memory_space=pltpu.SMEM)


ROWS = ((0,), (0,))
INNER = ((1,), (0,))


def halves(x):
    high = x.astype(jnp.bfloat16)
    return high, (x - high.astype(jnp.float32)).astype(jnp.bfloat16)


def product(a, b, contract):
    ((at,), (bt,)) = contract
    left = jnp.concatenate([a[0], a[0], a[1]], axis=at)
    right = jnp.concatenate([b[0], b[1], b[0]], axis=bt)
    return lax.dot_general(left, right, (contract, ((), ())), preferred_element_type=jnp.float32)


def split_table(table):
    high = np.asarray(table).astype(jnp.bfloat16)
    low = (table - high.astype(np.float64)).astype(jnp.bfloat16)
    return high, low


def first_table(upper):
    a = 2 * np.arange(64) + upper
    ang = (a[:, None] * np.arange(128)[None, :] % 128) * (2 * math.pi / 128)
    cos, sin = np.cos(ang), np.sin(ang)
    return split_table(np.block([[cos, sin], [-sin, cos]]))


def turn_table(half):
    ang = (np.arange(128)[:, None] + 128 * half) * np.arange(128)[None, :] * (2 * math.pi / 32768)
    return np.stack([np.cos(ang), np.sin(ang)]).astype(np.float32)


def second_table(half):
    m = np.arange(128) + 128 * half
    ang = (np.arange(256)[:, None] * m[None] % 256) * (2 * math.pi / 256)
    cos, sin = np.cos(ang) / 32768, np.sin(ang) / 32768
    real = np.concatenate([cos, -sin], axis=1)
    imag = np.concatenate([sin, cos], axis=1)
    return split_table(np.stack([real, imag], axis=1).reshape(512, 256))


def groups_of(chunk):
    return tuple(dict.fromkeys(g for g, _ in chunk))


def regroup_kernel(x_hbm, *refs):
    out_refs, x_ref, sems = refs[:-2], refs[-2], refs[-1]
    copies = []
    for n in range(4):
        rows = pl.ds(1024 * n, 1024)
        copies.append(pltpu.make_async_copy(x_hbm.at[rows], x_ref.at[rows], sems.at[n]))
        copies[n].start()
    for n in range(4):
        copies[n].wait()
        for index, chunk in enumerate(CHUNKS):
            head, rest = out_refs[2 * index], out_refs[2 * index + 1]
            for at, (g, c) in enumerate(chunk):
                lanes = pl.ds(128 * at, 128)

                def take(first, count):
                    return x_ref[pl.ds(8 * first + 2 * g + c, count, stride=8), :]

                if n == 0:
                    head[0:128, lanes] = take(0, 128)
                elif n == 1:
                    head[128:HEAD, lanes] = take(128, HEAD - 128)
                    rest[0 : 256 - HEAD, lanes] = take(HEAD, 256 - HEAD)
                else:
                    start = 128 * n - HEAD
                    rest[start : start + 128, lanes] = take(128 * n, 128)


def regroup(flat):
    shapes = []
    for chunk in CHUNKS:
        shapes.append(jax.ShapeDtypeStruct((HEAD, 128 * len(chunk)), jnp.float32))
        shapes.append(jax.ShapeDtypeStruct((512 - HEAD, 128 * len(chunk)), jnp.float32))
    return pl.pallas_call(
        regroup_kernel,
        out_shape=shapes,
        in_specs=[pl.BlockSpec(memory_space=pltpu.HBM)],
        out_specs=[VMEM] * len(shapes),
        scratch_shapes=[pltpu.VMEM((4096, 128), jnp.float32), pltpu.SemaphoreType.DMA((4,))],
        name="regroup",
        compiler_params=ROOM,
    )(flat)


def remap_kernel(chunk, src_ref, off_ref, w_ref, a0, b0, a1, b1, a2, before_ref, out_ref, energy_ref, ext):
    energy = before_ref[...]
    ext[0:HEAD, :] = a0[...]
    ext[HEAD:512, :] = b0[...]
    ext[512 : 512 + HEAD, :] = a1[...]
    ext[512 + HEAD : 1024, :] = b1[...]
    ext[1024 : 1024 + HEAD, :] = a2[...]
    ext[1024 + HEAD :, :] = jnp.zeros((WIN - HEAD, ext.shape[1]), jnp.float32)
    rows = lax.broadcasted_iota(jnp.int32, (WIN, BLOCK), 0)
    for which, group in enumerate(groups_of(chunk)):
        units = [at for at, (g, _) in enumerate(chunk) if g == group]
        lanes = slice(128 * units[0], 128 * units[-1] + 128)
        for b in range(4):
            start = pl.multiple_of(src_ref[which, b] * BLOCK, BLOCK)
            source = ext[pl.ds(start, WIN), lanes]
            here = pl.ds(b * BLOCK, BLOCK)
            tap_at = rows - off_ref[which, :, here]
            weights = jnp.zeros((WIN, BLOCK), jnp.float32)
            for t in range(TAPS):
                weights = jnp.where(tap_at == t, w_ref[which, pl.ds(t, 1), here], weights)
            result = product(halves(weights), halves(source), ROWS)
            for n, at in enumerate(units):
                part = result[:, 128 * n : 128 * n + 128].reshape(16, 8, 128)
                out_ref[pl.ds(16 * b, 16), at] = part
                energy = energy + jnp.sum(part * part, axis=0)
    energy_ref[...] = energy


def remap(chunk, src, off, weights, parts, before):
    return pl.pallas_call(
        lambda *refs: remap_kernel(chunk, *refs),
        out_shape=[
            jax.ShapeDtypeStruct((64, len(chunk), 8, 128), jnp.float32),
            jax.ShapeDtypeStruct((8, 128), jnp.float32),
        ],
        in_specs=[SMEM] + [VMEM] * 8,
        out_specs=[VMEM, VMEM],
        scratch_shapes=[pltpu.VMEM((1024 + WIN, 128 * len(chunk)), jnp.float32)],
        compiler_params=ROOM,
    )(src, off, weights, *parts, before)


def pack_kernel(x_ref, energy_ref, out_ref):
    count = x_ref.shape[1]
    rows = 8 * count + 1
    total = jnp.full((1, 128), jnp.sum(energy_ref[...]), jnp.float32)
    for a in range(64):
        for at in range(count):
            out_ref[pl.ds(rows * a + 8 * at, 8), :] = x_ref[a, at]
        out_ref[pl.ds(rows * a + rows - 1, 1), :] = total


def pack(x, energy):
    return pl.pallas_call(
        pack_kernel,
        out_shape=jax.ShapeDtypeStruct((64 * (8 * x.shape[1] + 1), 128), jnp.float32),
        in_specs=[VMEM, VMEM],
        out_specs=VMEM,
        name="pack",
        compiler_params=ROOM,
    )(x, energy)


def columns(pieces, rows):
    lanes = []
    for r in rows:
        parts = [ref[pl.ds(8 * at + r, 64, stride=ref.shape[0] // 64), :] for ref, at in pieces]
        lanes.append(jnp.concatenate(parts, axis=0))
    return halves(jnp.concatenate(lanes, axis=1))


def turned(step, cos, sin):
    lanes = []
    for r in range(step.shape[0] // 128):
        real, imag = step[128 * r : 128 * r + 128, :128], step[128 * r : 128 * r + 128, 128:]
        both = [real * cos - imag * sin, real * sin + imag * cos]
        lanes.append(jnp.concatenate(both, axis=0))
    return halves(jnp.concatenate(lanes, axis=1))


def early_kernel(x0, x1, fah, fal, fbh, fbl, turn, mh, ml, step_ref, part_ref):
    step_ref[...] = product(columns([(x1, 2)], range(8)), (fah[...], fal[...]), ROWS)
    for i in range(4):
        pieces = [(x1, 0), (x1, 1), (x0, 0), (x0, 1)]
        step = product(columns(pieces, (2 * i, 2 * i + 1)), (fbh[...], fbl[...]), ROWS)
        data = turned(step, turn[0], turn[1])
        part_ref[:, pl.ds(256 * i, 256)] = product((mh[...], ml[...]), data, INNER)


def early(x0, x1, tables):
    return pl.pallas_call(
        early_kernel,
        out_shape=[
            jax.ShapeDtypeStruct((1024, 256), jnp.float32),
            jax.ShapeDtypeStruct((512, 1024), jnp.float32),
        ],
        in_specs=[VMEM] * 9,
        out_specs=[VMEM, VMEM],
        name="early",
        compiler_params=ROOM,
    )(x0, x1, *tables)


def finish_kernel(*refs):
    sources, out_hbm, held = refs[:8], refs[8], refs[9:17]
    out_ref, load_sems, store_sems = refs[17:]
    x2, fh, fl, step_ref, turn, mh, ml, part_ref = held
    loads = [
        pltpu.make_async_copy(source, here, load_sems.at[n])
        for n, (source, here) in enumerate(zip(sources[:7], held[:7]))
    ]
    for i in range(4):
        lanes = pl.ds(256 * i, 256)
        loads.append(
            pltpu.make_async_copy(
                sources[7].at[:, lanes], part_ref.at[:, lanes], load_sems.at[7 + i]
            )
        )
    for copy in loads:
        copy.start()
    for copy in loads[:5]:
        copy.wait()
    energy = jnp.sum(x2[pl.ds(24, 64, stride=25), :], axis=0, keepdims=True)
    scale = lax.rsqrt(energy * (1.0 / (32768.0 * 134217728.0)) + 1e-06)
    pieces = [(x2, 0), (x2, 1), (x2, 2)]
    stores = []
    for i in range(4):
        moved = product(columns(pieces, (2 * i, 2 * i + 1)), (fh[...], fl[...]), ROWS)
        data = turned(step_ref[pl.ds(256 * i, 256), :] + moved, turn[0], turn[1])
        if i == 0:
            loads[5].wait()
            loads[6].wait()
        result = product((mh[...], ml[...]), data, INNER)
        loads[7 + i].wait()
        result = result + part_ref[:, pl.ds(256 * i, 256)]
        for at in range(2):
            out_ref[2 * i + at] = result[:, 128 * at : 128 * at + 128] * scale
        pair = pl.ds(2 * i, 2)
        stores.append(pltpu.make_async_copy(out_ref.at[pair], out_hbm.at[pair], store_sems.at[i]))
        stores[i].start()
    for copy in stores:
        copy.wait()


def finish(x2, step, part, tables):
    fh, fl, turn, mh, ml = tables
    operands = (x2, fh, fl, step, turn, mh, ml, part)
    return pl.pallas_call(
        finish_kernel,
        out_shape=jax.ShapeDtypeStruct((8, 512, 128), jnp.float32),
        in_specs=[ANY] * 8,
        out_specs=ANY,
        scratch_shapes=[pltpu.VMEM(x.shape, x.dtype) for x in operands]
        + [
            pltpu.VMEM((8, 512, 128), jnp.float32),
            pltpu.SemaphoreType.DMA((11,)),
            pltpu.SemaphoreType.DMA((4,)),
        ],
        name="finish",
        compiler_params=pltpu.CompilerParams(vmem_limit_bytes=FULL),
    )(*operands)


def steps(spectrum, src_block, offsets, tap_weights):
    position = lax.axis_index("rng")
    size = lax.axis_size("rng")
    down = [(i, i - 1) for i in range(1, size)]
    flat = spectrum.reshape(512, 2, 4, GW).transpose(0, 2, 1, 3).reshape(4096, GW)
    local = regroup(flat)
    src = jnp.clip(src_block - 4 * position, 0, 8)
    off = offsets.reshape(4, 1, 512)
    weights = tap_weights.transpose(1, 0, 2)

    def pull(x):
        return lax.ppermute(x, "rng", down)

    def swap(x):
        return lax.all_to_all(x, AZ, split_axis=0, concat_axis=0, tiled=True)

    energy = jnp.zeros((8, 128), jnp.float32)
    moved = []
    for i, chunk in enumerate(CHUNKS):
        near, far = local[2 * i], local[2 * i + 1]
        near_up = pull(near)
        far_up = pull(far)
        near_up_up = pull(near_up)

        def of_chunk(x):
            return jnp.concatenate([x[g : g + 1] for g in groups_of(chunk)], axis=0)

        out, energy = remap(
            chunk,
            of_chunk(src),
            of_chunk(off),
            of_chunk(weights),
            (near, far, near_up, far_up, near_up_up),
            energy,
        )
        moved.append(out)
    got0 = swap(moved[0]).reshape(-1, 128)
    got1 = swap(moved[1]).reshape(-1, 128)
    energy = lax.psum(energy, "rng")
    packed = pack(moved[2], energy)
    got2 = swap(packed.reshape(64, 1, -1)).reshape(packed.shape)
    lower, upper = first_table(0), first_table(1)
    first = [x[:64] for x in lower]
    second = [np.concatenate([x, y]) for x, y in zip(lower, upper)]
    third = [np.concatenate([x[64:], y]) for x, y in zip(lower, upper)]
    step, part = early(got0, got1, (*first, *second, turn_table(1), *second_table(1)))
    out = finish(got2, step, part, (*third, turn_table(0), *second_table(0)))
    return out.reshape(8, 256, 2, 128).transpose(0, 2, 1, 3).reshape(8, 2, 32768)


def solution(mesh):
    torus = Mesh(mesh.devices.reshape(mesh.shape["rng"], 8, 4, 2), RNG_AZ)
    placed = (P("rng", None, AZ), P(AZ, "rng"), P(AZ, "rng"), P(None, AZ, "rng"))
    return jax.shard_map(
        steps, mesh=torus, in_specs=placed, out_specs=P(RNG_AZ, None, None), check_vma=False
    )
```

time: 169 us -> 173 us (1.024)
  waiting for transfers between devices: 77.9 us -> 85.1 us
  Pallas kernels: 15.9 us -> 14.1 us
    all_to_all x3, waiting for transfers between devices: 11.9 us -> 19.2 us  [swap(): return lax.all_to_all(x, AZ, split_axis=0, concat_axis=0, tiled=True)]
where the time goes in v2:
time: 173 us
  waiting for transfers between devices  85.1 us (49%)
  starting transfers between devices  53.5 us (31%)
  blocking collectives  15.5 us (9%)
  Pallas kernels  14.1 us (8%)
  local copies, waits for them, and re-layouts  4.01 us (2%)
    ppermute x9, waiting for transfers between devices, pull(): return lax.ppermute(x, 'rng', down)  65.9 us
    all_to_all x3, starting transfers between devices, swap(): return lax.all_to_all(x, AZ, split_axis=0, concat_axis=0, tiled=True)  41.9 us
    all_to_all x3, waiting for transfers between devices, swap(): return lax.all_to_all(x, AZ, split_axis=0, concat_axis=0, tiled=True)  19.2 us
    psum x1, blocking collectives, steps(): energy = lax.psum(energy, 'rng')  15.5 us
    ppermute x9, starting transfers between devices, pull(): return lax.ppermute(x, 'rng', down)  11.6 us
    pallas_call x3, Pallas kernels, remap(): pl.pallas_call(lambda *refs: remap_kernel(chunk, *refs), out_shape=[jax.S...  5.45 us
    pallas_call x1, Pallas kernels, finish(): pl.pallas_call(finish_kernel, out_shape=jax.ShapeDtypeStruct((8, 512, 128...  5.04 us
    unnamed x27, local copies, waits for them, and re-layouts  3.98 us
  transfers between devices with their start and end apart: 12, of which 7 were waited for; matrix products, arithmetic and copies ran while one was open for 0% of the time, Pallas kernels for 4%

profile of v2, /device:TPU:1, one launch (start us, length us, event | category | flops | bytes accessed | tf_op | source)
XLA Modules:
  0.0 172.5 jit_solution(18168087054478827909)
XLA Ops:
  0.0 1.6 copy-done
  2.2 1.3 collective-permute-start.6
  3.5 1.3 collective-permute-start.7
  4.9 4.5 %collective-permute-done.6.refs_5_ = f32[136,256]{1,0:T(8,128)S(1)} collective-permute-done((f32[136,256]{1,0:T(8,128)S(1)}, f32[136,256]{1,0:T(8,128)S(1)}, u32[]{:S(2)}, u32[]{:S(2)}) %collective-permute-start.6) | collective-permute-done | bytes 139296 | tf_op jit(solution)/shard_map/ppermute | solution.py:291
  10.7 7.8 %collective-permute-done.8.refs_7_ = f32[136,256]{1,0:T(8,128)S(1)} collective-permute-done((f32[136,256]{1,0:T(8,128)S(1)}, f32[136,256]{1,0:T(8,128)S(1)}, u32[]{:S(2)}, u32[]{:S(2)}) %collective-permute-start.8) | collective-permute-done | bytes 139296 | tf_op jit(solution)/shard_map/ppermute | solution.py:291
  18.5 1.8 %shard_map.154 = (f32[64,2,8,128]{3,2,1,0:T(8,128)}, f32[8,128]{1,0:T(8,128)S(1)}) custom-call(s32[1,4]{1,0:T(1,128)S(1)} %get-tuple-element.43.refs_0_, s32[1,1,512]{2,1,0:T(1,128)S(1)} %get-tuple-element.39.refs_1_, f32[1,8,512]{2,1,0:T(8,128)S(1)} %get-tuple-element.33.refs_2_, f32[136,256]{1,0:T(8,128)S(1)} %get-tuple-element.23.refs_3_, ...), custom_call_target="tpu_custom_call" | custom-call | tf_op jit(solution)/shard_map/pallas_call | solution.py:146
  20.4 14.4 %all-to-all-start.1 = ((f32[64,2,8,128]{3,2,1,0:T(8,128)}), f32[64,2,8,128]{3,2,1,0:T(8,128)S(1)}, u32[]{:S(2)}, u32[]{:S(2)}) async-start(f32[64,2,8,128]{3,2,1,0:T(8,128)} %get-tuple-element.29), calls=%async_computation.1 | async-start | bytes 1048576 | tf_op jit(solution)/shard_map/all_to_all | solution.py:294
  34.8 1.3 collective-permute-start.4
  36.1 1.3 collective-permute-start.3
  37.4 18.8 %collective-permute-done.3.refs_5_ = f32[136,384]{1,0:T(8,128)S(1)} collective-permute-done((f32[136,384]{1,0:T(8,128)S(1)}, f32[136,384]{1,0:T(8,128)S(1)}, u32[]{:S(2)}, u32[]{:S(2)}) %collective-permute-start.3) | collective-permute-done | bytes 208928 | tf_op jit(solution)/shard_map/ppermute | solution.py:291
  57.6 7.2 %collective-permute-done.5.refs_7_ = f32[136,384]{1,0:T(8,128)S(1)} collective-permute-done((f32[136,384]{1,0:T(8,128)S(1)}, f32[136,384]{1,0:T(8,128)S(1)}, u32[]{:S(2)}, u32[]{:S(2)}) %collective-permute-start.5) | collective-permute-done | bytes 208928 | tf_op jit(solution)/shard_map/ppermute | solution.py:291
  64.8 2.2 %shard_map.155 = (f32[64,3,8,128]{3,2,1,0:T(8,128)}, f32[8,128]{1,0:T(8,128)S(1)}) custom-call(s32[2,4]{1,0:T(2,128)S(1)} %get-tuple-element.49.refs_0_, s32[2,1,512]{2,1,0:T(1,128)S(1)} %get-tuple-element.47.refs_1_, f32[2,8,512]{2,1,0:T(8,128)S(1)} %get-tuple-element.37.refs_2_, f32[136,384]{1,0:T(8,128)S(1)} %get-tuple-element.21.refs_3_, ...), custom_call_target="tpu_custom_call" | custom-call | tf_op jit(solution)/shard_map/pallas_call | solution.py:146
  67.0 11.6 %all-to-all-start.2 = ((f32[64,3,8,128]{3,2,1,0:T(8,128)}), f32[64,3,8,128]{3,2,1,0:T(8,128)S(1)}, u32[]{:S(2)}, u32[]{:S(2)}) async-start(f32[64,3,8,128]{3,2,1,0:T(8,128)} %get-tuple-element.30), calls=%async_computation.2 | async-start | bytes 1572864 | tf_op jit(solution)/shard_map/all_to_all | solution.py:294
  78.6 1.3 collective-permute-start.1
  79.9 1.3 collective-permute-start
  81.2 20.1 %collective-permute-done.refs_5_ = f32[136,384]{1,0:T(8,128)S(1)} collective-permute-done((f32[136,384]{1,0:T(8,128)S(1)}, f32[136,384]{1,0:T(8,128)S(1)}, u32[]{:S(2)}, u32[]{:S(2)}) %collective-permute-start) | collective-permute-done | bytes 208928 | tf_op jit(solution)/shard_map/ppermute | solution.py:291
  102.5 7.5 %collective-permute-done.2.refs_7_ = f32[136,384]{1,0:T(8,128)S(1)} collective-permute-done((f32[136,384]{1,0:T(8,128)S(1)}, f32[136,384]{1,0:T(8,128)S(1)}, u32[]{:S(2)}, u32[]{:S(2)}) %collective-permute-start.2) | collective-permute-done | bytes 208928 | tf_op jit(solution)/shard_map/ppermute | solution.py:291
  110.0 1.4 shard_map.156
  111.5 15.5 %psum.7.energy_ref = f32[8,128]{1,0:T(8,128)S(1)} all-reduce(f32[8,128]{1,0:T(8,128)S(1)} %get-tuple-element.28), channel_id=1, replica_groups=mesh['rng'=8,'az_0'=8,'az_1'=4,'az_2'=2] {'rng'}, use_global_device_ids=true, to_apply=%region_0.1 | all-reduce | flops 1024 | bytes 8192 | tf_op jit(solution)/shard_map/psum | solution.py:318
  128.0 15.9 %all-to-all-start = ((f32[64,1,3200]{2,1,0:T(1,128)}), f32[64,1,3200]{2,1,0:T(1,128)}, u32[]{:S(2)}, u32[]{:S(2)}) async-start(f32[64,1,3200]{2,1,0:T(1,128)} %bitcast.8), calls=%async_computation | async-start | bytes 1638400 | tf_op jit(solution)/shard_map/all_to_all | solution.py:294
  143.9 2.0 %early.1 = (f32[1024,256]{1,0:T(8,128)S(1)}, f32[512,1024]{1,0:T(8,128)S(1)}) custom-call(f32[1024,128]{1,0:T(8,128)S(1)} %bitcast.27, f32[1536,128]{1,0:T(8,128)S(1)} %bitcast.25, bf16[64,256]{1,0:T(8,128)(2,1)S(1)} %copy-done.9, bf16[64,256]{1,0:T(8,128)(2,1)S(1)} %copy-done.8, bf16[256,256]{1,0:T(8,128)(2,1)S(1)} %copy-done.7, ...), custom_call_target="tpu_custom_call" | custom-call | tf_op jit(solution)/shard_map/early/pallas_call | solution.py:207
  146.0 1.3 copy-done.1
  148.3 19.1 %all-to-all-done = f32[64,1,3200]{2,1,0:T(1,128)} async-done(((f32[64,1,3200]{2,1,0:T(1,128)}), f32[64,1,3200]{2,1,0:T(1,128)}, u32[]{:S(2)}, u32[]{:S(2)}) %all-to-all-start) | async-done | bytes 819232 | tf_op jit(solution)/shard_map/all_to_all | solution.py:294
  167.5 5.0 %finish.1 = f32[8,512,128]{2,1,0:T(8,128)} custom-call(f32[1600,128]{1,0:T(8,128)} %bitcast.9.refs_0_, bf16[192,256]{1,0:T(8,128)(2,1)} %constant.45.clone.refs_1_, bf16[192,256]{1,0:T(8,128)(2,1)} %constant.46.clone.refs_2_, f32[1024,256]{1,0:T(8,128)} %copy-done.2, f32[2,128,128]{2,1,0:T(8,128)} %constant.47.clone.refs_4_, ...), custom_call_target="tpu_custom_call" | custom-call | tf_op jit(solution)/shard_map/finish/pallas_call | solution.py:264
  (43 shorter events, 6.6 us)
Async XLA Ops:
  0.0 1.6 copy-start
  1.6 3.2 %copy-start.11 = (s32[4,512]{1,0:T(4,128)S(1)}, s32[4,512]{1,0:T(4,128)}, u32[]{:S(2)}) copy-start(s32[4,512]{1,0:T(4,128)} %param.18) | copy-start | bytes 24580
  1.6 3.2 %copy-start.10 = (f32[8,4,512]{2,1,0:T(4,128)S(1)}, f32[8,4,512]{2,1,0:T(4,128)}, u32[]{:S(2)}) copy-start(f32[8,4,512]{2,1,0:T(4,128)} %param.19) | copy-start | bytes 196612
  1.6 3.3 %copy-start.12 = (s32[4,4]{1,0:T(4,128)S(1)}, s32[4,4]{1,0:T(4,128)}, u32[]{:S(2)}) copy-start(s32[4,4]{1,0:T(4,128)} %param.17) | copy-start | bytes 196
  2.2 7.3 %collective-permute-start.6 = (f32[136,256]{1,0:T(8,128)S(1)}, f32[136,256]{1,0:T(8,128)S(1)}, u32[]{:S(2)}, u32[]{:S(2)}) collective-permute-start(f32[136,256]{1,0:T(8,128)S(1)} %get-tuple-element.23.refs_3_), channel_id=1, source_target_pairs={{64,0},{128,64},{192,128},{256,192},{320,256},{384,320},{448,384},... | collective-permute-start | bytes 417800 | tf_op jit(solution)/shard_map/ppermute | solution.py:291
  3.5 15.1 %collective-permute-start.7 = (f32[376,256]{1,0:T(8,128)S(1)}, f32[376,256]{1,0:T(8,128)S(1)}, u32[]{:S(2)}, u32[]{:S(2)}) collective-permute-start(f32[376,256]{1,0:T(8,128)S(1)} %get-tuple-element.24.refs_4_), channel_id=1, source_target_pairs={{64,0},{128,64},{192,128},{256,192},{320,256},{384,320},{448,384},... | collective-permute-start | bytes 1155080 | tf_op jit(solution)/shard_map/ppermute | solution.py:291
  9.4 9.1 %collective-permute-start.8 = (f32[136,256]{1,0:T(8,128)S(1)}, f32[136,256]{1,0:T(8,128)S(1)}, u32[]{:S(2)}, u32[]{:S(2)}) collective-permute-start(f32[136,256]{1,0:T(8,128)S(1)} %collective-permute-done.6.refs_5_), channel_id=1, source_target_pairs={{64,0},{128,64},{192,128},{256,192},{320,256},{384,320},{448,384},... | collective-permute-start | bytes 417800 | tf_op jit(solution)/shard_map/ppermute | solution.py:291
  20.4 46.6 %all-to-all-start.1 = ((f32[64,2,8,128]{3,2,1,0:T(8,128)}), f32[64,2,8,128]{3,2,1,0:T(8,128)S(1)}, u32[]{:S(2)}, u32[]{:S(2)}) async-start(f32[64,2,8,128]{3,2,1,0:T(8,128)} %get-tuple-element.29), calls=%async_computation.1 | async-start | bytes 1048576 | tf_op jit(solution)/shard_map/all_to_all | solution.py:294
  34.8 30.0 %collective-permute-start.4 = (f32[376,384]{1,0:T(8,128)S(1)}, f32[376,384]{1,0:T(8,128)S(1)}, u32[]{:S(2)}, u32[]{:S(2)}) collective-permute-start(f32[376,384]{1,0:T(8,128)S(1)} %get-tuple-element.22.refs_4_), channel_id=1, source_target_pairs={{64,0},{128,64},{192,128},{256,192},{320,256},{384,320},{448,384},... | collective-permute-start | bytes 1732616 | tf_op jit(solution)/shard_map/ppermute | solution.py:291
  36.1 20.2 %collective-permute-start.3 = (f32[136,384]{1,0:T(8,128)S(1)}, f32[136,384]{1,0:T(8,128)S(1)}, u32[]{:S(2)}, u32[]{:S(2)}) collective-permute-start(f32[136,384]{1,0:T(8,128)S(1)} %get-tuple-element.21.refs_3_), channel_id=1, source_target_pairs={{64,0},{128,64},{192,128},{256,192},{320,256},{384,320},{448,384},... | collective-permute-start | bytes 626696 | tf_op jit(solution)/shard_map/ppermute | solution.py:291
  56.3 8.5 %collective-permute-start.5 = (f32[136,384]{1,0:T(8,128)S(1)}, f32[136,384]{1,0:T(8,128)S(1)}, u32[]{:S(2)}, u32[]{:S(2)}) collective-permute-start(f32[136,384]{1,0:T(8,128)S(1)} %collective-permute-done.3.refs_5_), channel_id=1, source_target_pairs={{64,0},{128,64},{192,128},{256,192},{320,256},{384,320},{448,384},... | collective-permute-start | bytes 626696 | tf_op jit(solution)/shard_map/ppermute | solution.py:291
  67.0 61.0 %all-to-all-start.2 = ((f32[64,3,8,128]{3,2,1,0:T(8,128)}), f32[64,3,8,128]{3,2,1,0:T(8,128)S(1)}, u32[]{:S(2)}, u32[]{:S(2)}) async-start(f32[64,3,8,128]{3,2,1,0:T(8,128)} %get-tuple-element.30), calls=%async_computation.2 | async-start | bytes 1572864 | tf_op jit(solution)/shard_map/all_to_all | solution.py:294
  78.6 31.5 %collective-permute-start.1 = (f32[376,384]{1,0:T(8,128)S(1)}, f32[376,384]{1,0:T(8,128)S(1)}, u32[]{:S(2)}, u32[]{:S(2)}) collective-permute-start(f32[376,384]{1,0:T(8,128)S(1)} %get-tuple-element.20.refs_4_), channel_id=1, source_target_pairs={{64,0},{128,64},{192,128},{256,192},{320,256},{384,320},{448,384},... | collective-permute-start | bytes 1732616 | tf_op jit(solution)/shard_map/ppermute | solution.py:291
  79.9 21.4 %collective-permute-start = (f32[136,384]{1,0:T(8,128)S(1)}, f32[136,384]{1,0:T(8,128)S(1)}, u32[]{:S(2)}, u32[]{:S(2)}) collective-permute-start(f32[136,384]{1,0:T(8,128)S(1)} %get-tuple-element.19.refs_3_), channel_id=1, source_target_pairs={{64,0},{128,64},{192,128},{256,192},{320,256},{384,320},{448,384},... | collective-permute-start | bytes 626696 | tf_op jit(solution)/shard_map/ppermute | solution.py:291
  101.2 8.8 %collective-permute-start.2 = (f32[136,384]{1,0:T(8,128)S(1)}, f32[136,384]{1,0:T(8,128)S(1)}, u32[]{:S(2)}, u32[]{:S(2)}) collective-permute-start(f32[136,384]{1,0:T(8,128)S(1)} %collective-permute-done.refs_5_), channel_id=1, source_target_pairs={{64,0},{128,64},{192,128},{256,192},{320,256},{384,320},{448,384},... | collective-permute-start | bytes 626696 | tf_op jit(solution)/shard_map/ppermute | solution.py:291
  110.0 33.9 %copy-start.3 = (bf16[512,256]{1,0:T(8,128)(2,1)S(1)}, bf16[512,256]{1,0:T(8,128)(2,1)}, u32[]{:S(2)}) copy-start(bf16[512,256]{1,0:T(8,128)(2,1)} %constant.44.clone.ml) | copy-start | bytes 786436
  110.0 33.9 %copy-start.4 = (bf16[512,256]{1,0:T(8,128)(2,1)S(1)}, bf16[512,256]{1,0:T(8,128)(2,1)}, u32[]{:S(2)}) copy-start(bf16[512,256]{1,0:T(8,128)(2,1)} %constant.43.clone.mh) | copy-start | bytes 786436
  110.0 33.9 %copy-start.8 = (bf16[64,256]{1,0:T(8,128)(2,1)S(1)}, bf16[64,256]{1,0:T(8,128)(2,1)}, u32[]{:S(2)}) copy-start(bf16[64,256]{1,0:T(8,128)(2,1)} %constant.39.clone.fal) | copy-start | bytes 98308
  110.0 33.9 %copy-start.9 = (bf16[64,256]{1,0:T(8,128)(2,1)S(1)}, bf16[64,256]{1,0:T(8,128)(2,1)}, u32[]{:S(2)}) copy-start(bf16[64,256]{1,0:T(8,128)(2,1)} %constant.38.clone.fah) | copy-start | bytes 98308
  111.5 32.5 %copy-start.5 = (f32[2,128,128]{2,1,0:T(8,128)S(1)}, f32[2,128,128]{2,1,0:T(8,128)}, u32[]{:S(2)}) copy-start(f32[2,128,128]{2,1,0:T(8,128)} %constant.42.clone.turn) | copy-start | bytes 393220
  111.5 32.5 %copy-start.6 = (bf16[256,256]{1,0:T(8,128)(2,1)S(1)}, bf16[256,256]{1,0:T(8,128)(2,1)}, u32[]{:S(2)}) copy-start(bf16[256,256]{1,0:T(8,128)(2,1)} %constant.41.clone.fbl) | copy-start | bytes 393220
  111.5 32.5 %copy-start.7 = (bf16[256,256]{1,0:T(8,128)(2,1)S(1)}, bf16[256,256]{1,0:T(8,128)(2,1)}, u32[]{:S(2)}) copy-start(bf16[256,256]{1,0:T(8,128)(2,1)} %constant.40.clone.fbh) | copy-start | bytes 393220
  128.0 39.5 %all-to-all-start = ((f32[64,1,3200]{2,1,0:T(1,128)}), f32[64,1,3200]{2,1,0:T(1,128)}, u32[]{:S(2)}, u32[]{:S(2)}) async-start(f32[64,1,3200]{2,1,0:T(1,128)} %bitcast.8), calls=%async_computation | async-start | bytes 1638400 | tf_op jit(solution)/shard_map/all_to_all | solution.py:294
  146.0 1.3 copy-start.1
  (1 other events, 1.0 us)

commit v3 on v1

--- a/solution.py
+++ b/solution.py
@@ -20,6 +20,7 @@
 FULL = 63 << 20
 ROOM = pltpu.CompilerParams(vmem_limit_bytes=12 << 20)
 VMEM = pl.BlockSpec(memory_space=pltpu.VMEM)
+ANY = pl.BlockSpec(memory_space=pl.ANY)
 SMEM = pl.BlockSpec(memory_space=pltpu.SMEM)
 
 
@@ -29,13 +30,10 @@
 
 
 def product(a, b, contract):
-    a_high, a_low = a
-    b_high, b_low = b
-
-    def times(x, y):
-        return lax.dot_general(x, y, (contract, ((), ())), preferred_element_type=jnp.float32)
-
-    return times(a_high, b_high) + times(a_high, b_low) + times(a_low, b_high)
+    ((at,), (bt,)) = contract
+    left = jnp.concatenate([a[0], a[0], a[1]], axis=at)
+    right = jnp.concatenate([b[0], b[1], b[0]], axis=bt)
+    return lax.dot_general(left, right, (contract, ((), ())), preferred_element_type=jnp.float32)
 
 
 def split_table(table):
@@ -65,14 +63,32 @@
     return split_table(np.stack([real, imag], axis=1).reshape(512, 256))
 
 
-def regroup_kernel(x_ref, *out_refs):
-    for index, chunk in enumerate(CHUNKS):
-        head, rest = out_refs[2 * index], out_refs[2 * index + 1]
-        for at, g in enumerate(chunk):
-            for c in range(2):
-                lanes = pl.ds(128 * c, 128)
-                head[at, :, lanes] = x_ref[pl.ds(2 * g + c, HEAD, stride=8), :]
-                rest[at, :, lanes] = x_ref[pl.ds(8 * HEAD + 2 * g + c, 512 - HEAD, stride=8), :]
+def regroup_kernel(x_hbm, *refs):
+    out_refs, x_ref, sems = refs[:-2], refs[-2], refs[-1]
+    copies = []
+    for n in range(4):
+        rows = pl.ds(1024 * n, 1024)
+        copies.append(pltpu.make_async_copy(x_hbm.at[rows], x_ref.at[rows], sems.at[n]))
+        copies[n].start()
+    for n in range(4):
+        copies[n].wait()
+        for index, chunk in enumerate(CHUNKS):
+            head, rest = out_refs[2 * index], out_refs[2 * index + 1]
+            for at, g in enumerate(chunk):
+                for c in range(2):
+                    lanes = pl.ds(128 * c, 128)
+
+                    def take(first, count):
+                        return x_ref[pl.ds(8 * first + 2 * g + c, count, stride=8), :]
+
+                    if n == 0:
+                        head[at, 0:128, lanes] = take(0, 128)
+                    elif n == 1:
+                        head[at, 128:HEAD, lanes] = take(128, HEAD - 128)
+                        rest[at, 0 : 256 - HEAD, lanes] = take(HEAD, 256 - HEAD)
+                    else:
+                        start = 128 * n - HEAD
+                        rest[at, start : start + 128, lanes] = take(128 * n, 128)
 
 
 def regroup(flat):
@@ -83,6 +99,9 @@
     return pl.pallas_call(
         regroup_kernel,
         out_shape=shapes,
+        in_specs=[pl.BlockSpec(memory_space=pltpu.HBM)],
+        out_specs=[VMEM] * len(shapes),
+        scratch_shapes=[pltpu.VMEM((4096, 128), jnp.float32), pltpu.SemaphoreType.DMA((4,))],
         name="regroup",
         compiler_params=ROOM,
     )(flat)
@@ -203,37 +222,65 @@
     )(x0, x13, *tables)
 
 
-def finish_kernel(x2, step_ref, part_ref, f1h, f1l, turn, mh, ml, out_ref):
-    i = pl.program_id(0)
+def finish_kernel(*refs):
+    sources, out_hbm, held = refs[:8], refs[8], refs[9:17]
+    out_ref, load_sems, store_sems = refs[17:]
+    x2, fh, fl, turn, mh, ml, step_ref, part_ref = held
+    pairs = [(source, here) for source, here in zip(sources[:6], held[:6])]
+    for i in range(4):
+        rows = pl.ds(256 * i, 256)
+        pairs.append((sources[6].at[rows], step_ref.at[rows]))
+    for i in range(4):
+        lanes = pl.ds(256 * i, 256)
+        pairs.append((sources[7].at[:, lanes], part_ref.at[:, lanes]))
+    loads = [
+        pltpu.make_async_copy(source, here, load_sems.at[n])
+        for n, (source, here) in enumerate(pairs)
+    ]
+    for n in (0, 1, 2, 6, 3, 4, 5, 10, 7, 11, 8, 12, 9, 13):
+        loads[n].start()
+    for copy in loads[:4]:
+        copy.wait()
     energy = jnp.sum(x2[pl.ds(16, 64, stride=17), :], axis=0, keepdims=True)
     scale = lax.rsqrt(energy * (1.0 / (32768.0 * 134217728.0)) + 1e-06)
-    step = step_ref[...] + product(
-        columns(x2, 0, 17, (2 * i, 2 * i + 1)), (f1h[...], f1l[...]), ROWS
-    )
-    data = turned(step, turn[0], turn[1])
-    result = part_ref[...] + product((mh[...], ml[...]), data, INNER)
-    for at in range(2):
-        out_ref[at] = result[:, 128 * at : 128 * at + 128] * scale
+    stores = []
+    for i in range(4):
+        pair = (2 * i, 2 * i + 1)
+        moved = product(columns(x2, 0, 17, pair), (fh[...], fl[...]), ROWS)
+        loads[6 + i].wait()
+        data = turned(step_ref[pl.ds(256 * i, 256), :] + moved, turn[0], turn[1])
+        if i == 0:
+            loads[4].wait()
+            loads[5].wait()
+        result = product((mh[...], ml[...]), data, INNER)
+        loads[10 + i].wait()
+        result = result + part_ref[:, pl.ds(256 * i, 256)]
+        for at in range(2):
+            out_ref[2 * i + at] = result[:, 128 * at : 128 * at + 128] * scale
+        both = pl.ds(2 * i, 2)
+        stores.append(pltpu.make_async_copy(out_ref.at[both], out_hbm.at[both], store_sems.at[i]))
+        stores[i].start()
+    for copy in stores:
+        copy.wait()
 
 
 def finish(x2, step, part, tables):
-    def whole(shape):
-        return pl.BlockSpec(shape, lambda i: (0,) * len(shape))
-
+    fh, fl, turn, mh, ml = tables
+    operands = (x2, fh, fl, turn, mh, ml, step, part)
     return pl.pallas_call(
         finish_kernel,
         out_shape=jax.ShapeDtypeStruct((8, 512, 128), jnp.float32),
-        grid=(4,),
-        in_specs=[
-            whole((1088, 128)),
-            pl.BlockSpec((256, 256), lambda i: (i, 0)),
-            pl.BlockSpec((512, 256), lambda i: (0, i)),
-        ]
-        + [whole(t.shape) for t in tables],
-        out_specs=pl.BlockSpec((2, 512, 128), lambda i: (i, 0, 0)),
+        in_specs=[ANY] * 8,
+        out_specs=ANY,
+        scratch_shapes=[pltpu.VMEM(x.shape, x.dtype) for x in operands]
+        + [
+            pltpu.VMEM((8, 512, 128), jnp.float32),
+            pltpu.SemaphoreType.DMA((14,)),
+            pltpu.SemaphoreType.DMA((4,)),
+        ],
         name="finish",
         compiler_params=pltpu.CompilerParams(vmem_limit_bytes=FULL),
-    )(x2, step, part, *tables)
+    )(*operands)
 
 
 def steps(spectrum, src_block, offsets, tap_weights):

time: 169 us -> 168 us (level)
  no operation moved by 1% of the time
where the time goes in v3:
time: 168 us; the launch traced here: 167 us
  waiting for transfers between devices  78.1 us (46%)
  starting transfers between devices  53.7 us (32%)
  blocking collectives  15.4 us (9%)
  Pallas kernels  14.6 us (9%)
  local copies, waits for them, and re-layouts  4.86 us (3%)
    ppermute x9, waiting for transfers between devices, pull(): return lax.ppermute(x, 'rng', down)  65.9 us
    all_to_all x3, starting transfers between devices, swap(): return lax.all_to_all(x, AZ, split_axis=0, concat_axis=0, tiled=True)  42 us
    psum x1, blocking collectives, steps(): energy = lax.psum(energy, 'rng')  15.4 us
    all_to_all x3, waiting for transfers between devices, swap(): return lax.all_to_all(x, AZ, split_axis=0, concat_axis=0, tiled=True)  12.2 us
    ppermute x9, starting transfers between devices, pull(): return lax.ppermute(x, 'rng', down)  11.7 us
    pallas_call x3, Pallas kernels, remap(): pl.pallas_call(remap_kernel, out_shape=[jax.ShapeDtypeStruct((64, count,...  5.22 us
    pallas_call x1, Pallas kernels, finish(): pl.pallas_call(finish_kernel, out_shape=jax.ShapeDtypeStruct((8, 512, 128...  5.02 us
    unnamed x27, local copies, waits for them, and re-layouts  4.84 us
  transfers between devices with their start and end apart: 12, of which 7 were waited for; matrix products, arithmetic and copies ran while one was open for 0% of the time, Pallas kernels for 4%

profile of v3, /device:TPU:1, one launch (start us, length us, event | category | flops | bytes accessed | tf_op | source)
XLA Modules:
  0.0 167.1 jit_solution(13384482467745376200)
XLA Ops:
  0.0 1.6 copy-done.1
  2.2 1.3 collective-permute-start.6
  3.5 1.3 collective-permute-start.7
  4.9 4.5 %collective-permute-done.6.a1 = f32[1,136,256]{2,1,0:T(8,128)S(1)} collective-permute-done((f32[1,136,256]{2,1,0:T(8,128)S(1)}, f32[1,136,256]{2,1,0:T(8,128)S(1)}, u32[]{:S(2)}, u32[]{:S(2)}) %collective-permute-start.6) | collective-permute-done | bytes 139296 | tf_op jit(solution)/shard_map/ppermute | solution.py:297
  10.7 7.8 %collective-permute-done.8.a2 = f32[1,136,256]{2,1,0:T(8,128)S(1)} collective-permute-done((f32[1,136,256]{2,1,0:T(8,128)S(1)}, f32[1,136,256]{2,1,0:T(8,128)S(1)}, u32[]{:S(2)}, u32[]{:S(2)}) %collective-permute-start.8) | collective-permute-done | bytes 139296 | tf_op jit(solution)/shard_map/ppermute | solution.py:297
  18.5 1.8 %shard_map.136 = (f32[64,1,2,8,128]{4,3,2,1,0:T(8,128)}, f32[8,128]{1,0:T(8,128)S(1)}) custom-call(s32[1,4]{1,0:T(1,128)S(1)} %get-tuple-element.41.src_ref, s32[1,1,512]{2,1,0:T(1,128)S(1)} %get-tuple-element.37.off_ref, f32[1,8,512]{2,1,0:T(8,128)S(1)} %get-tuple-element.33.w_ref, f32[1,136,256]{2,1,0:T(8,128)S(1)} %get-tuple-element.23.a0, ...), custom_call_target="tpu_custom_call" | custom-call | tf_op jit(solution)/shard_map/pallas_call | solution.py:146
  20.4 14.4 %all-to-all-start.1 = ((f32[64,1,2,8,128]{4,3,2,1,0:T(8,128)}), f32[64,1,2,8,128]{4,3,2,1,0:T(8,128)S(1)}, u32[]{:S(2)}, u32[]{:S(2)}) async-start(f32[64,1,2,8,128]{4,3,2,1,0:T(8,128)} %get-tuple-element.29), calls=%async_computation.1 | async-start | bytes 1048576 | tf_op jit(solution)/shard_map/all_to_all | solution.py:300
  34.8 1.3 collective-permute-start.4
  36.1 1.3 collective-permute-start.3
  37.4 24.5 %collective-permute-done.3.a1 = f32[2,136,256]{2,1,0:T(8,128)S(1)} collective-permute-done((f32[2,136,256]{2,1,0:T(8,128)S(1)}, f32[2,136,256]{2,1,0:T(8,128)S(1)}, u32[]{:S(2)}, u32[]{:S(2)}) %collective-permute-start.3) | collective-permute-done | bytes 278560 | tf_op jit(solution)/shard_map/ppermute | solution.py:297
  61.9 1.3 collective-permute-start.5
  63.2 8.7 %collective-permute-done.5.a2 = f32[2,136,256]{2,1,0:T(8,128)S(1)} collective-permute-done((f32[2,136,256]{2,1,0:T(8,128)S(1)}, f32[2,136,256]{2,1,0:T(8,128)S(1)}, u32[]{:S(2)}, u32[]{:S(2)}) %collective-permute-start.5) | collective-permute-done | bytes 278560 | tf_op jit(solution)/shard_map/ppermute | solution.py:297
  71.9 2.4 %shard_map.137 = (f32[64,2,2,8,128]{4,3,2,1,0:T(8,128)}, f32[8,128]{1,0:T(8,128)S(1)}) custom-call(s32[2,4]{1,0:T(2,128)S(1)} %pad_add_fusion.1.src_ref, s32[2,1,512]{2,1,0:T(1,128)S(1)} %pad_add_fusion.off_ref, f32[2,8,512]{2,1,0:T(8,128)S(1)} %pad_maximum_fusion.w_ref, f32[2,136,256]{2,1,0:T(8,128)S(1)} %get-tuple-element.21.a0, ...), custom_call_target="tpu_custom_call" | custom-call | tf_op jit(solution)/shard_map/pallas_call | solution.py:146
  74.2 11.6 %all-to-all-start.2 = ((f32[64,2,2,8,128]{4,3,2,1,0:T(8,128)}), f32[64,2,2,8,128]{4,3,2,1,0:T(8,128)S(1)}, u32[]{:S(2)}, u32[]{:S(2)}) async-start(f32[64,2,2,8,128]{4,3,2,1,0:T(8,128)} %get-tuple-element.30), calls=%async_computation.2 | async-start | bytes 2097152 | tf_op jit(solution)/shard_map/all_to_all | solution.py:300
  85.9 1.4 collective-permute-start.1
  87.3 1.3 collective-permute-start
  88.6 14.5 %collective-permute-done.a1 = f32[1,136,256]{2,1,0:T(8,128)S(1)} collective-permute-done((f32[1,136,256]{2,1,0:T(8,128)S(1)}, f32[1,136,256]{2,1,0:T(8,128)S(1)}, u32[]{:S(2)}, u32[]{:S(2)}) %collective-permute-start) | collective-permute-done | bytes 139296 | tf_op jit(solution)/shard_map/ppermute | solution.py:297
  104.4 6.0 %collective-permute-done.2.a2 = f32[1,136,256]{2,1,0:T(8,128)S(1)} collective-permute-done((f32[1,136,256]{2,1,0:T(8,128)S(1)}, f32[1,136,256]{2,1,0:T(8,128)S(1)}, u32[]{:S(2)}, u32[]{:S(2)}) %collective-permute-start.2) | collective-permute-done | bytes 139296 | tf_op jit(solution)/shard_map/ppermute | solution.py:297
  111.4 15.4 %psum.7.energy_ref = f32[8,128]{1,0:T(8,128)S(1)} all-reduce(f32[8,128]{1,0:T(8,128)S(1)} %get-tuple-element.28), channel_id=1, replica_groups=mesh['rng'=8,'az_0'=8,'az_1'=4,'az_2'=2] {'rng'}, use_global_device_ids=true, to_apply=%region_0.1 | all-reduce | flops 1024 | bytes 8192 | tf_op jit(solution)/shard_map/psum | solution.py:323
  127.8 16.0 %all-to-all-start = ((f32[64,1,2176]{2,1,0:T(1,128)}), f32[64,1,2176]{2,1,0:T(1,128)}, u32[]{:S(2)}, u32[]{:S(2)}) async-start(f32[64,1,2176]{2,1,0:T(1,128)} %bitcast.8), calls=%async_computation | async-start | bytes 1114112 | tf_op jit(solution)/shard_map/all_to_all | solution.py:300
  144.7 2.9 %early.1 = (f32[1024,256]{1,0:T(8,128)S(1)}, f32[512,1024]{1,0:T(8,128)S(1)}) custom-call(f32[1024,128]{1,0:T(8,128)S(1)} %bitcast.26, f32[2048,128]{1,0:T(8,128)S(1)} %bitcast.25, bf16[128,256]{1,0:T(8,128)(2,1)S(1)} %copy-done.9, bf16[128,256]{1,0:T(8,128)(2,1)S(1)} %copy-done.8, bf16[128,256]{1,0:T(8,128)(2,1)S(1)} %copy-done.4, ...), custom_call_target="tpu_custom_call" | custom-call | tf_op jit(solution)/shard_map/early/pallas_call | solution.py:212
  147.6 1.3 copy-done
  149.9 12.2 %all-to-all-done = f32[64,1,2176]{2,1,0:T(1,128)} async-done(((f32[64,1,2176]{2,1,0:T(1,128)}), f32[64,1,2176]{2,1,0:T(1,128)}, u32[]{:S(2)}, u32[]{:S(2)}) %all-to-all-start) | async-done | bytes 557088 | tf_op jit(solution)/shard_map/all_to_all | solution.py:300
  162.1 5.0 %finish.1 = f32[8,512,128]{2,1,0:T(8,128)} custom-call(f32[1088,128]{1,0:T(8,128)} %bitcast.9.refs_0_, bf16[128,256]{1,0:T(8,128)(2,1)} %constant.36.clone.f1h.refs_1_, bf16[128,256]{1,0:T(8,128)(2,1)} %constant.37.clone.f1l.refs_2_, f32[2,128,128]{2,1,0:T(8,128)} %constant.41.clone.refs_3_, bf16[512,256]{1,0:T(8,128)(2,1)} %constant.42.clone.refs_4_, ...), custom_call_target="tpu_custom_call" | custom-call | tf_op jit(solution)/shard_map/finish/pallas_call | solution.py:270
  (43 shorter events, 7.1 us)
Async XLA Ops:
  0.0 1.6 copy-start.1
  1.6 3.2 %copy-start.11 = (s32[4,512]{1,0:T(4,128)S(1)}, s32[4,512]{1,0:T(4,128)}, u32[]{:S(2)}) copy-start(s32[4,512]{1,0:T(4,128)} %param.16) | copy-start | bytes 24580
  1.6 3.2 %copy-start.10 = (f32[8,4,512]{2,1,0:T(4,128)S(1)}, f32[8,4,512]{2,1,0:T(4,128)}, u32[]{:S(2)}) copy-start(f32[8,4,512]{2,1,0:T(4,128)} %param.17) | copy-start | bytes 196612
  1.6 3.3 %copy-start.12 = (s32[4,4]{1,0:T(4,128)S(1)}, s32[4,4]{1,0:T(4,128)}, u32[]{:S(2)}) copy-start(s32[4,4]{1,0:T(4,128)} %param.15) | copy-start | bytes 196
  2.2 7.3 %collective-permute-start.6 = (f32[1,136,256]{2,1,0:T(8,128)S(1)}, f32[1,136,256]{2,1,0:T(8,128)S(1)}, u32[]{:S(2)}, u32[]{:S(2)}) collective-permute-start(f32[1,136,256]{2,1,0:T(8,128)S(1)} %get-tuple-element.23.a0), channel_id=1, source_target_pairs={{64,0},{128,64},{192,128},{256,192},{320,256},{384,320},{448,384},... | collective-permute-start | bytes 417800 | tf_op jit(solution)/shard_map/ppermute | solution.py:297
  3.5 15.1 %collective-permute-start.7 = (f32[1,376,256]{2,1,0:T(8,128)S(1)}, f32[1,376,256]{2,1,0:T(8,128)S(1)}, u32[]{:S(2)}, u32[]{:S(2)}) collective-permute-start(f32[1,376,256]{2,1,0:T(8,128)S(1)} %get-tuple-element.24.b0), channel_id=1, source_target_pairs={{64,0},{128,64},{192,128},{256,192},{320,256},{384,320},{448,384},... | collective-permute-start | bytes 1155080 | tf_op jit(solution)/shard_map/ppermute | solution.py:297
  9.4 9.1 %collective-permute-start.8 = (f32[1,136,256]{2,1,0:T(8,128)S(1)}, f32[1,136,256]{2,1,0:T(8,128)S(1)}, u32[]{:S(2)}, u32[]{:S(2)}) collective-permute-start(f32[1,136,256]{2,1,0:T(8,128)S(1)} %collective-permute-done.6.a1), channel_id=1, source_target_pairs={{64,0},{128,64},{192,128},{256,192},{320,256},{384,320},{448,384},... | collective-permute-start | bytes 417800 | tf_op jit(solution)/shard_map/ppermute | solution.py:297
  20.4 53.9 %all-to-all-start.1 = ((f32[64,1,2,8,128]{4,3,2,1,0:T(8,128)}), f32[64,1,2,8,128]{4,3,2,1,0:T(8,128)S(1)}, u32[]{:S(2)}, u32[]{:S(2)}) async-start(f32[64,1,2,8,128]{4,3,2,1,0:T(8,128)} %get-tuple-element.29), calls=%async_computation.1 | async-start | bytes 1048576 | tf_op jit(solution)/shard_map/all_to_all | solution.py:300
  34.8 37.1 %collective-permute-start.4 = (f32[2,376,256]{2,1,0:T(8,128)S(1)}, f32[2,376,256]{2,1,0:T(8,128)S(1)}, u32[]{:S(2)}, u32[]{:S(2)}) collective-permute-start(f32[2,376,256]{2,1,0:T(8,128)S(1)} %get-tuple-element.22.b0), channel_id=1, source_target_pairs={{64,0},{128,64},{192,128},{256,192},{320,256},{384,320},{448,384},... | collective-permute-start | bytes 2310152 | tf_op jit(solution)/shard_map/ppermute | solution.py:297
  36.1 25.8 %collective-permute-start.3 = (f32[2,136,256]{2,1,0:T(8,128)S(1)}, f32[2,136,256]{2,1,0:T(8,128)S(1)}, u32[]{:S(2)}, u32[]{:S(2)}) collective-permute-start(f32[2,136,256]{2,1,0:T(8,128)S(1)} %get-tuple-element.21.a0), channel_id=1, source_target_pairs={{64,0},{128,64},{192,128},{256,192},{320,256},{384,320},{448,384},... | collective-permute-start | bytes 835592 | tf_op jit(solution)/shard_map/ppermute | solution.py:297
  61.9 10.0 %collective-permute-start.5 = (f32[2,136,256]{2,1,0:T(8,128)S(1)}, f32[2,136,256]{2,1,0:T(8,128)S(1)}, u32[]{:S(2)}, u32[]{:S(2)}) collective-permute-start(f32[2,136,256]{2,1,0:T(8,128)S(1)} %collective-permute-done.3.a1), channel_id=1, source_target_pairs={{64,0},{128,64},{192,128},{256,192},{320,256},{384,320},{448,384},... | collective-permute-start | bytes 835592 | tf_op jit(solution)/shard_map/ppermute | solution.py:297
  74.2 53.6 %all-to-all-start.2 = ((f32[64,2,2,8,128]{4,3,2,1,0:T(8,128)}), f32[64,2,2,8,128]{4,3,2,1,0:T(8,128)S(1)}, u32[]{:S(2)}, u32[]{:S(2)}) async-start(f32[64,2,2,8,128]{4,3,2,1,0:T(8,128)} %get-tuple-element.30), calls=%async_computation.2 | async-start | bytes 2097152 | tf_op jit(solution)/shard_map/all_to_all | solution.py:300
  85.8 58.0 %copy-start.3 = (bf16[128,256]{1,0:T(8,128)(2,1)S(1)}, bf16[128,256]{1,0:T(8,128)(2,1)}, u32[]{:S(2)}) copy-start(bf16[128,256]{1,0:T(8,128)(2,1)} %constant.37.clone.f1l.refs_2_) | copy-start | bytes 196612
  85.8 58.0 %copy-start.4 = (bf16[128,256]{1,0:T(8,128)(2,1)S(1)}, bf16[128,256]{1,0:T(8,128)(2,1)}, u32[]{:S(2)}) copy-start(bf16[128,256]{1,0:T(8,128)(2,1)} %constant.36.clone.f1h.refs_1_) | copy-start | bytes 196612
  85.8 58.0 %copy-start.5 = (bf16[512,256]{1,0:T(8,128)(2,1)S(1)}, bf16[512,256]{1,0:T(8,128)(2,1)}, u32[]{:S(2)}) copy-start(bf16[512,256]{1,0:T(8,128)(2,1)} %constant.40.clone.ml) | copy-start | bytes 786436
  85.8 58.0 %copy-start.6 = (bf16[512,256]{1,0:T(8,128)(2,1)S(1)}, bf16[512,256]{1,0:T(8,128)(2,1)}, u32[]{:S(2)}) copy-start(bf16[512,256]{1,0:T(8,128)(2,1)} %constant.39.clone.mh) | copy-start | bytes 786436
  85.9 58.0 %copy-start.7 = (f32[2,128,128]{2,1,0:T(8,128)S(1)}, f32[2,128,128]{2,1,0:T(8,128)}, u32[]{:S(2)}) copy-start(f32[2,128,128]{2,1,0:T(8,128)} %constant.38.clone.turn) | copy-start | bytes 393220
  85.9 58.0 %copy-start.8 = (bf16[128,256]{1,0:T(8,128)(2,1)S(1)}, bf16[128,256]{1,0:T(8,128)(2,1)}, u32[]{:S(2)}) copy-start(bf16[128,256]{1,0:T(8,128)(2,1)} %constant.35.clone.f0l) | copy-start | bytes 196612
  85.9 24.5 %collective-permute-start.1 = (f32[1,376,256]{2,1,0:T(8,128)S(1)}, f32[1,376,256]{2,1,0:T(8,128)S(1)}, u32[]{:S(2)}, u32[]{:S(2)}) collective-permute-start(f32[1,376,256]{2,1,0:T(8,128)S(1)} %get-tuple-element.20.b0), channel_id=1, source_target_pairs={{64,0},{128,64},{192,128},{256,192},{320,256},{384,320},{448,384},... | collective-permute-start | bytes 1155080 | tf_op jit(solution)/shard_map/ppermute | solution.py:297
  87.3 15.8 %collective-permute-start = (f32[1,136,256]{2,1,0:T(8,128)S(1)}, f32[1,136,256]{2,1,0:T(8,128)S(1)}, u32[]{:S(2)}, u32[]{:S(2)}) collective-permute-start(f32[1,136,256]{2,1,0:T(8,128)S(1)} %get-tuple-element.19.a0), channel_id=1, source_target_pairs={{64,0},{128,64},{192,128},{256,192},{320,256},{384,320},{448,384},... | collective-permute-start | bytes 417800 | tf_op jit(solution)/shard_map/ppermute | solution.py:297
  103.1 7.3 %collective-permute-start.2 = (f32[1,136,256]{2,1,0:T(8,128)S(1)}, f32[1,136,256]{2,1,0:T(8,128)S(1)}, u32[]{:S(2)}, u32[]{:S(2)}) collective-permute-start(f32[1,136,256]{2,1,0:T(8,128)S(1)} %collective-permute-done.a1), channel_id=1, source_target_pairs={{64,0},{128,64},{192,128},{256,192},{320,256},{384,320},{448,384},... | collective-permute-start | bytes 417800 | tf_op jit(solution)/shard_map/ppermute | solution.py:297
  127.8 34.3 %all-to-all-start = ((f32[64,1,2176]{2,1,0:T(1,128)}), f32[64,1,2176]{2,1,0:T(1,128)}, u32[]{:S(2)}, u32[]{:S(2)}) async-start(f32[64,1,2176]{2,1,0:T(1,128)} %bitcast.8), calls=%async_computation | async-start | bytes 1114112 | tf_op jit(solution)/shard_map/all_to_all | solution.py:300
  147.6 1.4 copy-start
  149.0 1.0 copy-start.2
  (1 other events, 0.8 us)

commit v4 on v3

--- a/solution.py
+++ b/solution.py
@@ -107,11 +107,38 @@
     )(flat)
 
 
-def remap_kernel(src_ref, off_ref, w_ref, a0, b0, a1, b1, a2, before_ref, out_ref, energy_ref, ext):
+def place(off_ref, w_ref, at, b):
+    here = pl.ds(b * BLOCK, BLOCK)
+    tap_at = lax.broadcasted_iota(jnp.int32, (WIN, BLOCK), 0) - off_ref[at, :, here]
+    weights = jnp.zeros((WIN, BLOCK), jnp.float32)
+    for t in range(TAPS):
+        weights = jnp.where(tap_at == t, w_ref[at, pl.ds(t, 1), here], weights)
+    return halves(weights)
+
+
+def place_kernel(off_ref, w_ref, out_ref):
+    for at in range(off_ref.shape[0]):
+        for b in range(4):
+            for n, part in enumerate(place(off_ref, w_ref, at, b)):
+                out_ref[pl.ds(WIN * (8 * at + 2 * b + n), WIN), :] = part
+
+
+def placed(off, weights):
+    rows = off.shape[0] * 8 * WIN
+    return pl.pallas_call(
+        place_kernel,
+        out_shape=jax.ShapeDtypeStruct((rows, BLOCK), jnp.bfloat16),
+        in_specs=[VMEM, VMEM],
+        out_specs=VMEM,
+        name="place",
+        compiler_params=ROOM,
+    )(off, weights)
+
+
+def remap_kernel(ready, src_ref, off_ref, w_ref, a0, b0, a1, b1, a2, before_ref, out_ref, energy_ref, ext):
     count = a0.shape[0]
     energy = before_ref[...]
     ext[1024 + HEAD :, :] = jnp.zeros((ext.shape[0] - 1024 - HEAD, 256), jnp.float32)
-    rows = lax.broadcasted_iota(jnp.int32, (WIN, BLOCK), 0)
     for at in range(count):
         ext[0:HEAD, :] = a0[at]
         ext[HEAD:512, :] = b0[at]
@@ -121,12 +148,12 @@
         for b in range(4):
             start = pl.multiple_of(src_ref[at, b] * BLOCK, BLOCK)
             source = ext[pl.ds(start, WIN), :]
-            here = pl.ds(b * BLOCK, BLOCK)
-            tap_at = rows - off_ref[at, :, here]
-            weights = jnp.zeros((WIN, BLOCK), jnp.float32)
-            for t in range(TAPS):
-                weights = jnp.where(tap_at == t, w_ref[at, pl.ds(t, 1), here], weights)
-            w_high, w_low = halves(weights)
+            if ready:
+                first = WIN * (8 * at + 2 * b)
+                w_high = w_ref[pl.ds(first, WIN), :]
+                w_low = w_ref[pl.ds(first + WIN, WIN), :]
+            else:
+                w_high, w_low = place(off_ref, w_ref, at, b)
             s_high, s_low = halves(source)
             result = lax.dot_general(
                 jnp.concatenate([w_high, w_high, w_low], axis=0),
@@ -143,8 +170,9 @@
 
 def remap(src, off, weights, parts, before):
     count = off.shape[0]
-    return pl.pallas_call(
-        remap_kernel,
+    ready = weights.dtype == jnp.bfloat16
+    return pl.pallas_call(
+        lambda *refs: remap_kernel(ready, *refs),
         out_shape=[
             jax.ShapeDtypeStruct((64, count, 2, 8, 128), jnp.float32),
             jax.ShapeDtypeStruct((8, 128), jnp.float32),
@@ -310,12 +338,11 @@
         def of_chunk(x):
             return jnp.concatenate([x[g : g + 1] for g in chunk], axis=0)
 
+        off_here, weights_here = of_chunk(off), of_chunk(weights)
+        if i == 1:
+            weights_here = placed(off_here, weights_here)
         out, energy = remap(
-            of_chunk(src),
-            of_chunk(off),
-            of_chunk(weights),
-            (near, far, near_up, far_up, near_up_up),
-            energy,
+            of_chunk(src), off_here, weights_here, (near, far, near_up, far_up, near_up_up), energy
         )
         moved.append(out)
     got0 = swap(moved[0]).reshape(1024, 128)

time: 168 us -> 168 us (level)
    pallas_call x3 -> x4, Pallas kernels: 5.22 us -> 5.38 us  [the longest x3 4.99 us: remap(): pl.pallas_call(lambda *refs: remap_kernel(ready, *refs), out_shape=[jax.S...]
where the time goes in v4:
time: 168 us; the launch traced here: 167 us
  waiting for transfers between devices  77.7 us (46%)
  starting transfers between devices  53.7 us (32%)
  blocking collectives  15.4 us (9%)
  Pallas kernels  14.8 us (9%)
  local copies, waits for them, and re-layouts  4.86 us (3%)
    ppermute x9, waiting for transfers between devices, pull(): return lax.ppermute(x, 'rng', down)  65.5 us
    all_to_all x3, starting transfers between devices, swap(): return lax.all_to_all(x, AZ, split_axis=0, concat_axis=0, tiled=True)  42 us
    psum x1, blocking collectives, steps(): energy = lax.psum(energy, 'rng')  15.4 us
    all_to_all x3, waiting for transfers between devices, swap(): return lax.all_to_all(x, AZ, split_axis=0, concat_axis=0, tiled=True)  12.2 us
    ppermute x9, starting transfers between devices, pull(): return lax.ppermute(x, 'rng', down)  11.7 us
    pallas_call x1, Pallas kernels, finish(): pl.pallas_call(finish_kernel, out_shape=jax.ShapeDtypeStruct((8, 512, 128...  5.03 us
    pallas_call x3, Pallas kernels, remap(): pl.pallas_call(lambda *refs: remap_kernel(ready, *refs), out_shape=[jax.S...  4.99 us
    unnamed x27, local copies, waits for them, and re-layouts  4.84 us
  transfers between devices with their start and end apart: 12, of which 7 were waited for; matrix products, arithmetic and copies ran while one was open for 0% of the time, Pallas kernels for 4%

profile of v4, /device:TPU:1, one launch (start us, length us, event | category | flops | bytes accessed | tf_op | source)
XLA Modules:
  0.0 166.9 jit_solution(11613481987315333011)
XLA Ops:
  0.0 1.6 copy-done.1
  2.2 1.3 collective-permute-start.6
  3.5 1.3 collective-permute-start.7
  4.9 4.5 %collective-permute-done.6.refs_5_ = f32[1,136,256]{2,1,0:T(8,128)S(1)} collective-permute-done((f32[1,136,256]{2,1,0:T(8,128)S(1)}, f32[1,136,256]{2,1,0:T(8,128)S(1)}, u32[]{:S(2)}, u32[]{:S(2)}) %collective-permute-start.6) | collective-permute-done | bytes 139296 | tf_op jit(solution)/shard_map/ppermute | solution.py:325
  10.7 7.8 %collective-permute-done.8.refs_7_ = f32[1,136,256]{2,1,0:T(8,128)S(1)} collective-permute-done((f32[1,136,256]{2,1,0:T(8,128)S(1)}, f32[1,136,256]{2,1,0:T(8,128)S(1)}, u32[]{:S(2)}, u32[]{:S(2)}) %collective-permute-start.8) | collective-permute-done | bytes 139296 | tf_op jit(solution)/shard_map/ppermute | solution.py:325
  18.5 1.8 %shard_map.136 = (f32[64,1,2,8,128]{4,3,2,1,0:T(8,128)}, f32[8,128]{1,0:T(8,128)S(1)}) custom-call(s32[1,4]{1,0:T(1,128)S(1)} %get-tuple-element.41.refs_0_, s32[1,1,512]{2,1,0:T(1,128)S(1)} %get-tuple-element.37.refs_1_, f32[1,8,512]{2,1,0:T(8,128)S(1)} %get-tuple-element.33.refs_2_, f32[1,136,256]{2,1,0:T(8,128)S(1)} %get-tuple-element.23.refs_3_, ...), custom_call_target="tpu_custom_call" | custom-call | tf_op jit(solution)/shard_map/pallas_call | solution.py:174
  20.4 14.4 %all-to-all-start.1 = ((f32[64,1,2,8,128]{4,3,2,1,0:T(8,128)}), f32[64,1,2,8,128]{4,3,2,1,0:T(8,128)S(1)}, u32[]{:S(2)}, u32[]{:S(2)}) async-start(f32[64,1,2,8,128]{4,3,2,1,0:T(8,128)} %get-tuple-element.29), calls=%async_computation.1 | async-start | bytes 1048576 | tf_op jit(solution)/shard_map/all_to_all | solution.py:328
  34.8 1.3 collective-permute-start.4
  36.1 1.3 collective-permute-start.3
  37.4 24.5 %collective-permute-done.3.refs_5_ = f32[2,136,256]{2,1,0:T(8,128)S(1)} collective-permute-done((f32[2,136,256]{2,1,0:T(8,128)S(1)}, f32[2,136,256]{2,1,0:T(8,128)S(1)}, u32[]{:S(2)}, u32[]{:S(2)}) %collective-permute-start.3) | collective-permute-done | bytes 278560 | tf_op jit(solution)/shard_map/ppermute | solution.py:325
  61.9 1.3 collective-permute-start.5
  63.6 8.3 %collective-permute-done.5.refs_7_ = f32[2,136,256]{2,1,0:T(8,128)S(1)} collective-permute-done((f32[2,136,256]{2,1,0:T(8,128)S(1)}, f32[2,136,256]{2,1,0:T(8,128)S(1)}, u32[]{:S(2)}, u32[]{:S(2)}) %collective-permute-start.5) | collective-permute-done | bytes 278560 | tf_op jit(solution)/shard_map/ppermute | solution.py:325
  71.9 2.1 %shard_map.137 = (f32[64,2,2,8,128]{4,3,2,1,0:T(8,128)}, f32[8,128]{1,0:T(8,128)S(1)}) custom-call(s32[2,4]{1,0:T(2,128)S(1)} %pad_add_fusion.1.refs_0_, s32[2,1,512]{2,1,0:T(1,128)S(1)} %pad_add_fusion.off_ref.refs_1_, bf16[2304,128]{1,0:T(8,128)(2,1)S(1)} %place.1.refs_2_, f32[2,136,256]{2,1,0:T(8,128)S(1)} %get-tuple-element.21.refs_3_, ...), custom_call_target="tpu_custom_call" | custom-call | tf_op jit(solution)/shard_map/pallas_call | solution.py:174
  74.0 11.6 %all-to-all-start.2 = ((f32[64,2,2,8,128]{4,3,2,1,0:T(8,128)}), f32[64,2,2,8,128]{4,3,2,1,0:T(8,128)S(1)}, u32[]{:S(2)}, u32[]{:S(2)}) async-start(f32[64,2,2,8,128]{4,3,2,1,0:T(8,128)} %get-tuple-element.30), calls=%async_computation.2 | async-start | bytes 2097152 | tf_op jit(solution)/shard_map/all_to_all | solution.py:328
  85.7 1.4 collective-permute-start.1
  87.1 1.3 collective-permute-start
  88.4 14.5 %collective-permute-done.refs_5_ = f32[1,136,256]{2,1,0:T(8,128)S(1)} collective-permute-done((f32[1,136,256]{2,1,0:T(8,128)S(1)}, f32[1,136,256]{2,1,0:T(8,128)S(1)}, u32[]{:S(2)}, u32[]{:S(2)}) %collective-permute-start) | collective-permute-done | bytes 139296 | tf_op jit(solution)/shard_map/ppermute | solution.py:325
  104.1 6.0 %collective-permute-done.2.refs_7_ = f32[1,136,256]{2,1,0:T(8,128)S(1)} collective-permute-done((f32[1,136,256]{2,1,0:T(8,128)S(1)}, f32[1,136,256]{2,1,0:T(8,128)S(1)}, u32[]{:S(2)}, u32[]{:S(2)}) %collective-permute-start.2) | collective-permute-done | bytes 139296 | tf_op jit(solution)/shard_map/ppermute | solution.py:325
  111.2 15.4 %psum.7.energy_ref = f32[8,128]{1,0:T(8,128)S(1)} all-reduce(f32[8,128]{1,0:T(8,128)S(1)} %get-tuple-element.28), channel_id=1, replica_groups=mesh['rng'=8,'az_0'=8,'az_1'=4,'az_2'=2] {'rng'}, use_global_device_ids=true, to_apply=%region_0.1 | all-reduce | flops 1024 | bytes 8192 | tf_op jit(solution)/shard_map/psum | solution.py:350
  127.6 16.0 %all-to-all-start = ((f32[64,1,2176]{2,1,0:T(1,128)}), f32[64,1,2176]{2,1,0:T(1,128)}, u32[]{:S(2)}, u32[]{:S(2)}) async-start(f32[64,1,2176]{2,1,0:T(1,128)} %bitcast.8), calls=%async_computation | async-start | bytes 1114112 | tf_op jit(solution)/shard_map/all_to_all | solution.py:328
  144.5 2.9 %early.1 = (f32[1024,256]{1,0:T(8,128)S(1)}, f32[512,1024]{1,0:T(8,128)S(1)}) custom-call(f32[1024,128]{1,0:T(8,128)S(1)} %bitcast.26, f32[2048,128]{1,0:T(8,128)S(1)} %bitcast.25, bf16[128,256]{1,0:T(8,128)(2,1)S(1)} %copy-done.9, bf16[128,256]{1,0:T(8,128)(2,1)S(1)} %copy-done.8, bf16[128,256]{1,0:T(8,128)(2,1)S(1)} %copy-done.4, ...), custom_call_target="tpu_custom_call" | custom-call | tf_op jit(solution)/shard_map/early/pallas_call | solution.py:240
  147.4 1.3 copy-done
  149.7 12.2 %all-to-all-done = f32[64,1,2176]{2,1,0:T(1,128)} async-done(((f32[64,1,2176]{2,1,0:T(1,128)}), f32[64,1,2176]{2,1,0:T(1,128)}, u32[]{:S(2)}, u32[]{:S(2)}) %all-to-all-start) | async-done | bytes 557088 | tf_op jit(solution)/shard_map/all_to_all | solution.py:328
  161.9 5.0 %finish.1 = f32[8,512,128]{2,1,0:T(8,128)} custom-call(f32[1088,128]{1,0:T(8,128)} %bitcast.9.refs_0_, bf16[128,256]{1,0:T(8,128)(2,1)} %constant.36.clone.f1h.refs_1_, bf16[128,256]{1,0:T(8,128)(2,1)} %constant.37.clone.f1l.refs_2_, f32[2,128,128]{2,1,0:T(8,128)} %constant.41.clone.refs_3_, bf16[512,256]{1,0:T(8,128)(2,1)} %constant.42.clone.refs_4_, ...), custom_call_target="tpu_custom_call" | custom-call | tf_op jit(solution)/shard_map/finish/pallas_call | solution.py:298
  (44 shorter events, 7.5 us)
Async XLA Ops:
  0.0 1.6 copy-start.1
  1.6 3.2 %copy-start.11 = (s32[4,512]{1,0:T(4,128)S(1)}, s32[4,512]{1,0:T(4,128)}, u32[]{:S(2)}) copy-start(s32[4,512]{1,0:T(4,128)} %param.16) | copy-start | bytes 24580
  1.6 3.2 %copy-start.10 = (f32[8,4,512]{2,1,0:T(4,128)S(1)}, f32[8,4,512]{2,1,0:T(4,128)}, u32[]{:S(2)}) copy-start(f32[8,4,512]{2,1,0:T(4,128)} %param.17) | copy-start | bytes 196612
  1.6 3.3 %copy-start.12 = (s32[4,4]{1,0:T(4,128)S(1)}, s32[4,4]{1,0:T(4,128)}, u32[]{:S(2)}) copy-start(s32[4,4]{1,0:T(4,128)} %param.15) | copy-start | bytes 196
  2.2 7.3 %collective-permute-start.6 = (f32[1,136,256]{2,1,0:T(8,128)S(1)}, f32[1,136,256]{2,1,0:T(8,128)S(1)}, u32[]{:S(2)}, u32[]{:S(2)}) collective-permute-start(f32[1,136,256]{2,1,0:T(8,128)S(1)} %get-tuple-element.23.refs_3_), channel_id=1, source_target_pairs={{64,0},{128,64},{192,128},{256,192},{320,256},{384,320},{448,384},... | collective-permute-start | bytes 417800 | tf_op jit(solution)/shard_map/ppermute | solution.py:325
  3.5 15.1 %collective-permute-start.7 = (f32[1,376,256]{2,1,0:T(8,128)S(1)}, f32[1,376,256]{2,1,0:T(8,128)S(1)}, u32[]{:S(2)}, u32[]{:S(2)}) collective-permute-start(f32[1,376,256]{2,1,0:T(8,128)S(1)} %get-tuple-element.24.refs_4_), channel_id=1, source_target_pairs={{64,0},{128,64},{192,128},{256,192},{320,256},{384,320},{448,384},... | collective-permute-start | bytes 1155080 | tf_op jit(solution)/shard_map/ppermute | solution.py:325
  9.4 9.1 %collective-permute-start.8 = (f32[1,136,256]{2,1,0:T(8,128)S(1)}, f32[1,136,256]{2,1,0:T(8,128)S(1)}, u32[]{:S(2)}, u32[]{:S(2)}) collective-permute-start(f32[1,136,256]{2,1,0:T(8,128)S(1)} %collective-permute-done.6.refs_5_), channel_id=1, source_target_pairs={{64,0},{128,64},{192,128},{256,192},{320,256},{384,320},{448,384},... | collective-permute-start | bytes 417800 | tf_op jit(solution)/shard_map/ppermute | solution.py:325
  20.4 53.6 %all-to-all-start.1 = ((f32[64,1,2,8,128]{4,3,2,1,0:T(8,128)}), f32[64,1,2,8,128]{4,3,2,1,0:T(8,128)S(1)}, u32[]{:S(2)}, u32[]{:S(2)}) async-start(f32[64,1,2,8,128]{4,3,2,1,0:T(8,128)} %get-tuple-element.29), calls=%async_computation.1 | async-start | bytes 1048576 | tf_op jit(solution)/shard_map/all_to_all | solution.py:328
  34.8 37.1 %collective-permute-start.4 = (f32[2,376,256]{2,1,0:T(8,128)S(1)}, f32[2,376,256]{2,1,0:T(8,128)S(1)}, u32[]{:S(2)}, u32[]{:S(2)}) collective-permute-start(f32[2,376,256]{2,1,0:T(8,128)S(1)} %get-tuple-element.22.refs_4_), channel_id=1, source_target_pairs={{64,0},{128,64},{192,128},{256,192},{320,256},{384,320},{448,384},... | collective-permute-start | bytes 2310152 | tf_op jit(solution)/shard_map/ppermute | solution.py:325
  36.1 25.8 %collective-permute-start.3 = (f32[2,136,256]{2,1,0:T(8,128)S(1)}, f32[2,136,256]{2,1,0:T(8,128)S(1)}, u32[]{:S(2)}, u32[]{:S(2)}) collective-permute-start(f32[2,136,256]{2,1,0:T(8,128)S(1)} %get-tuple-element.21.refs_3_), channel_id=1, source_target_pairs={{64,0},{128,64},{192,128},{256,192},{320,256},{384,320},{448,384},... | collective-permute-start | bytes 835592 | tf_op jit(solution)/shard_map/ppermute | solution.py:325
  61.9 10.0 %collective-permute-start.5 = (f32[2,136,256]{2,1,0:T(8,128)S(1)}, f32[2,136,256]{2,1,0:T(8,128)S(1)}, u32[]{:S(2)}, u32[]{:S(2)}) collective-permute-start(f32[2,136,256]{2,1,0:T(8,128)S(1)} %collective-permute-done.3.refs_5_), channel_id=1, source_target_pairs={{64,0},{128,64},{192,128},{256,192},{320,256},{384,320},{448,384},... | collective-permute-start | bytes 835592 | tf_op jit(solution)/shard_map/ppermute | solution.py:325
  74.0 53.6 %all-to-all-start.2 = ((f32[64,2,2,8,128]{4,3,2,1,0:T(8,128)}), f32[64,2,2,8,128]{4,3,2,1,0:T(8,128)S(1)}, u32[]{:S(2)}, u32[]{:S(2)}) async-start(f32[64,2,2,8,128]{4,3,2,1,0:T(8,128)} %get-tuple-element.30), calls=%async_computation.2 | async-start | bytes 2097152 | tf_op jit(solution)/shard_map/all_to_all | solution.py:328
  85.6 58.0 %copy-start.3 = (bf16[128,256]{1,0:T(8,128)(2,1)S(1)}, bf16[128,256]{1,0:T(8,128)(2,1)}, u32[]{:S(2)}) copy-start(bf16[128,256]{1,0:T(8,128)(2,1)} %constant.37.clone.f1l.refs_2_) | copy-start | bytes 196612
  85.6 58.0 %copy-start.4 = (bf16[128,256]{1,0:T(8,128)(2,1)S(1)}, bf16[128,256]{1,0:T(8,128)(2,1)}, u32[]{:S(2)}) copy-start(bf16[128,256]{1,0:T(8,128)(2,1)} %constant.36.clone.f1h.refs_1_) | copy-start | bytes 196612
  85.6 58.0 %copy-start.5 = (bf16[512,256]{1,0:T(8,128)(2,1)S(1)}, bf16[512,256]{1,0:T(8,128)(2,1)}, u32[]{:S(2)}) copy-start(bf16[512,256]{1,0:T(8,128)(2,1)} %constant.40.clone.ml) | copy-start | bytes 786436
  85.6 58.0 %copy-start.6 = (bf16[512,256]{1,0:T(8,128)(2,1)S(1)}, bf16[512,256]{1,0:T(8,128)(2,1)}, u32[]{:S(2)}) copy-start(bf16[512,256]{1,0:T(8,128)(2,1)} %constant.39.clone.mh) | copy-start | bytes 786436
  85.6 58.0 %copy-start.7 = (f32[2,128,128]{2,1,0:T(8,128)S(1)}, f32[2,128,128]{2,1,0:T(8,128)}, u32[]{:S(2)}) copy-start(f32[2,128,128]{2,1,0:T(8,128)} %constant.38.clone.turn) | copy-start | bytes 393220
  85.6 58.0 %copy-start.8 = (bf16[128,256]{1,0:T(8,128)(2,1)S(1)}, bf16[128,256]{1,0:T(8,128)(2,1)}, u32[]{:S(2)}) copy-start(bf16[128,256]{1,0:T(8,128)(2,1)} %constant.35.clone.f0l) | copy-start | bytes 196612
  85.7 24.5 %collective-permute-start.1 = (f32[1,376,256]{2,1,0:T(8,128)S(1)}, f32[1,376,256]{2,1,0:T(8,128)S(1)}, u32[]{:S(2)}, u32[]{:S(2)}) collective-permute-start(f32[1,376,256]{2,1,0:T(8,128)S(1)} %get-tuple-element.20.refs_4_), channel_id=1, source_target_pairs={{64,0},{128,64},{192,128},{256,192},{320,256},{384,320},{448,384},... | collective-permute-start | bytes 1155080 | tf_op jit(solution)/shard_map/ppermute | solution.py:325
  87.1 15.8 %collective-permute-start = (f32[1,136,256]{2,1,0:T(8,128)S(1)}, f32[1,136,256]{2,1,0:T(8,128)S(1)}, u32[]{:S(2)}, u32[]{:S(2)}) collective-permute-start(f32[1,136,256]{2,1,0:T(8,128)S(1)} %get-tuple-element.19.refs_3_), channel_id=1, source_target_pairs={{64,0},{128,64},{192,128},{256,192},{320,256},{384,320},{448,384},... | collective-permute-start | bytes 417800 | tf_op jit(solution)/shard_map/ppermute | solution.py:325
  102.8 7.3 %collective-permute-start.2 = (f32[1,136,256]{2,1,0:T(8,128)S(1)}, f32[1,136,256]{2,1,0:T(8,128)S(1)}, u32[]{:S(2)}, u32[]{:S(2)}) collective-permute-start(f32[1,136,256]{2,1,0:T(8,128)S(1)} %collective-permute-done.refs_5_), channel_id=1, source_target_pairs={{64,0},{128,64},{192,128},{256,192},{320,256},{384,320},{448,384},... | collective-permute-start | bytes 417800 | tf_op jit(solution)/shard_map/ppermute | solution.py:325
  127.6 34.3 %all-to-all-start = ((f32[64,1,2176]{2,1,0:T(1,128)}), f32[64,1,2176]{2,1,0:T(1,128)}, u32[]{:S(2)}, u32[]{:S(2)}) async-start(f32[64,1,2176]{2,1,0:T(1,128)} %bitcast.8), calls=%async_computation | async-start | bytes 1114112 | tf_op jit(solution)/shard_map/all_to_all | solution.py:328
  147.4 1.4 copy-start
  148.7 1.0 copy-start.2
  (1 other events, 0.8 us)

commit v5 on v4

--- a/solution.py
+++ b/solution.py
@@ -284,10 +284,10 @@
         loads[10 + i].wait()
         result = result + part_ref[:, pl.ds(256 * i, 256)]
         for at in range(2):
-            out_ref[2 * i + at] = result[:, 128 * at : 128 * at + 128] * scale
-        both = pl.ds(2 * i, 2)
-        stores.append(pltpu.make_async_copy(out_ref.at[both], out_hbm.at[both], store_sems.at[i]))
-        stores[i].start()
+            r = 2 * i + at
+            out_ref[r] = result[:, 128 * at : 128 * at + 128] * scale
+            stores.append(pltpu.make_async_copy(out_ref.at[r], out_hbm.at[r], store_sems.at[r]))
+            stores[r].start()
     for copy in stores:
         copy.wait()
 
@@ -304,7 +304,7 @@
         + [
             pltpu.VMEM((8, 512, 128), jnp.float32),
             pltpu.SemaphoreType.DMA((14,)),
-            pltpu.SemaphoreType.DMA((4,)),
+            pltpu.SemaphoreType.DMA((8,)),
         ],
         name="finish",
         compiler_params=pltpu.CompilerParams(vmem_limit_bytes=FULL),

time: 168 us -> 168 us (level)
  no operation moved by 1% of the time
where the time goes in v5:
time: 168 us; the launch traced here: 167 us
  waiting for transfers between devices  77.7 us (46%)
  starting transfers between devices  53.7 us (32%)
  blocking collectives  15.4 us (9%)
  Pallas kernels  14.9 us (9%)
  local copies, waits for them, and re-layouts  4.86 us (3%)
    ppermute x9, waiting for transfers between devices, pull(): return lax.ppermute(x, 'rng', down)  65.5 us
    all_to_all x3, starting transfers between devices, swap(): return lax.all_to_all(x, AZ, split_axis=0, concat_axis=0, tiled=True)  42 us
    psum x1, blocking collectives, steps(): energy = lax.psum(energy, 'rng')  15.4 us
    all_to_all x3, waiting for transfers between devices, swap(): return lax.all_to_all(x, AZ, split_axis=0, concat_axis=0, tiled=True)  12.2 us
    ppermute x9, starting transfers between devices, pull(): return lax.ppermute(x, 'rng', down)  11.7 us
    pallas_call x1, Pallas kernels, finish(): pl.pallas_call(finish_kernel, out_shape=jax.ShapeDtypeStruct((8, 512, 128...  5.15 us
    pallas_call x3, Pallas kernels, remap(): pl.pallas_call(lambda *refs: remap_kernel(ready, *refs), out_shape=[jax.S...  4.99 us
    unnamed x27, local copies, waits for them, and re-layouts  4.84 us
  transfers between devices with their start and end apart: 12, of which 7 were waited for; matrix products, arithmetic and copies ran while one was open for 0% of the time, Pallas kernels for 4%

profile of v5, /device:TPU:1, one launch (start us, length us, event | category | flops | bytes accessed | tf_op | source)
XLA Modules:
  0.0 167.0 jit_solution(17775952869677582622)
XLA Ops:
  0.0 1.6 copy-done.1
  2.2 1.3 collective-permute-start.6
  3.5 1.3 collective-permute-start.7
  4.9 4.5 %collective-permute-done.6.refs_5_ = f32[1,136,256]{2,1,0:T(8,128)S(1)} collective-permute-done((f32[1,136,256]{2,1,0:T(8,128)S(1)}, f32[1,136,256]{2,1,0:T(8,128)S(1)}, u32[]{:S(2)}, u32[]{:S(2)}) %collective-permute-start.6) | collective-permute-done | bytes 139296 | tf_op jit(solution)/shard_map/ppermute | solution.py:325
  10.7 7.8 %collective-permute-done.8.refs_7_ = f32[1,136,256]{2,1,0:T(8,128)S(1)} collective-permute-done((f32[1,136,256]{2,1,0:T(8,128)S(1)}, f32[1,136,256]{2,1,0:T(8,128)S(1)}, u32[]{:S(2)}, u32[]{:S(2)}) %collective-permute-start.8) | collective-permute-done | bytes 139296 | tf_op jit(solution)/shard_map/ppermute | solution.py:325
  18.5 1.8 %shard_map.136 = (f32[64,1,2,8,128]{4,3,2,1,0:T(8,128)}, f32[8,128]{1,0:T(8,128)S(1)}) custom-call(s32[1,4]{1,0:T(1,128)S(1)} %get-tuple-element.41.refs_0_, s32[1,1,512]{2,1,0:T(1,128)S(1)} %get-tuple-element.37.refs_1_, f32[1,8,512]{2,1,0:T(8,128)S(1)} %get-tuple-element.33.refs_2_, f32[1,136,256]{2,1,0:T(8,128)S(1)} %get-tuple-element.23.refs_3_, ...), custom_call_target="tpu_custom_call" | custom-call | tf_op jit(solution)/shard_map/pallas_call | solution.py:174
  20.4 14.4 %all-to-all-start.1 = ((f32[64,1,2,8,128]{4,3,2,1,0:T(8,128)}), f32[64,1,2,8,128]{4,3,2,1,0:T(8,128)S(1)}, u32[]{:S(2)}, u32[]{:S(2)}) async-start(f32[64,1,2,8,128]{4,3,2,1,0:T(8,128)} %get-tuple-element.29), calls=%async_computation.1 | async-start | bytes 1048576 | tf_op jit(solution)/shard_map/all_to_all | solution.py:328
  34.8 1.3 collective-permute-start.4
  36.1 1.3 collective-permute-start.3
  37.4 24.5 %collective-permute-done.3.refs_5_ = f32[2,136,256]{2,1,0:T(8,128)S(1)} collective-permute-done((f32[2,136,256]{2,1,0:T(8,128)S(1)}, f32[2,136,256]{2,1,0:T(8,128)S(1)}, u32[]{:S(2)}, u32[]{:S(2)}) %collective-permute-start.3) | collective-permute-done | bytes 278560 | tf_op jit(solution)/shard_map/ppermute | solution.py:325
  61.9 1.3 collective-permute-start.5
  63.6 8.3 %collective-permute-done.5.refs_7_ = f32[2,136,256]{2,1,0:T(8,128)S(1)} collective-permute-done((f32[2,136,256]{2,1,0:T(8,128)S(1)}, f32[2,136,256]{2,1,0:T(8,128)S(1)}, u32[]{:S(2)}, u32[]{:S(2)}) %collective-permute-start.5) | collective-permute-done | bytes 278560 | tf_op jit(solution)/shard_map/ppermute | solution.py:325
  71.9 2.1 %shard_map.137 = (f32[64,2,2,8,128]{4,3,2,1,0:T(8,128)}, f32[8,128]{1,0:T(8,128)S(1)}) custom-call(s32[2,4]{1,0:T(2,128)S(1)} %pad_add_fusion.1.refs_0_, s32[2,1,512]{2,1,0:T(1,128)S(1)} %pad_add_fusion.off_ref.refs_1_, bf16[2304,128]{1,0:T(8,128)(2,1)S(1)} %place.1.refs_2_, f32[2,136,256]{2,1,0:T(8,128)S(1)} %get-tuple-element.21.refs_3_, ...), custom_call_target="tpu_custom_call" | custom-call | tf_op jit(solution)/shard_map/pallas_call | solution.py:174
  74.0 11.6 %all-to-all-start.2 = ((f32[64,2,2,8,128]{4,3,2,1,0:T(8,128)}), f32[64,2,2,8,128]{4,3,2,1,0:T(8,128)S(1)}, u32[]{:S(2)}, u32[]{:S(2)}) async-start(f32[64,2,2,8,128]{4,3,2,1,0:T(8,128)} %get-tuple-element.30), calls=%async_computation.2 | async-start | bytes 2097152 | tf_op jit(solution)/shard_map/all_to_all | solution.py:328
  85.7 1.4 collective-permute-start.1
  87.1 1.3 collective-permute-start
  88.4 14.5 %collective-permute-done.refs_5_ = f32[1,136,256]{2,1,0:T(8,128)S(1)} collective-permute-done((f32[1,136,256]{2,1,0:T(8,128)S(1)}, f32[1,136,256]{2,1,0:T(8,128)S(1)}, u32[]{:S(2)}, u32[]{:S(2)}) %collective-permute-start) | collective-permute-done | bytes 139296 | tf_op jit(solution)/shard_map/ppermute | solution.py:325
  104.1 6.0 %collective-permute-done.2.refs_7_ = f32[1,136,256]{2,1,0:T(8,128)S(1)} collective-permute-done((f32[1,136,256]{2,1,0:T(8,128)S(1)}, f32[1,136,256]{2,1,0:T(8,128)S(1)}, u32[]{:S(2)}, u32[]{:S(2)}) %collective-permute-start.2) | collective-permute-done | bytes 139296 | tf_op jit(solution)/shard_map/ppermute | solution.py:325
  111.2 15.4 %psum.7.energy_ref = f32[8,128]{1,0:T(8,128)S(1)} all-reduce(f32[8,128]{1,0:T(8,128)S(1)} %get-tuple-element.28), channel_id=1, replica_groups=mesh['rng'=8,'az_0'=8,'az_1'=4,'az_2'=2] {'rng'}, use_global_device_ids=true, to_apply=%region_0.1 | all-reduce | flops 1024 | bytes 8192 | tf_op jit(solution)/shard_map/psum | solution.py:350
  127.6 16.0 %all-to-all-start = ((f32[64,1,2176]{2,1,0:T(1,128)}), f32[64,1,2176]{2,1,0:T(1,128)}, u32[]{:S(2)}, u32[]{:S(2)}) async-start(f32[64,1,2176]{2,1,0:T(1,128)} %bitcast.8), calls=%async_computation | async-start | bytes 1114112 | tf_op jit(solution)/shard_map/all_to_all | solution.py:328
  144.5 2.9 %early.1 = (f32[1024,256]{1,0:T(8,128)S(1)}, f32[512,1024]{1,0:T(8,128)S(1)}) custom-call(f32[1024,128]{1,0:T(8,128)S(1)} %bitcast.26, f32[2048,128]{1,0:T(8,128)S(1)} %bitcast.25, bf16[128,256]{1,0:T(8,128)(2,1)S(1)} %copy-done.9, bf16[128,256]{1,0:T(8,128)(2,1)S(1)} %copy-done.8, bf16[128,256]{1,0:T(8,128)(2,1)S(1)} %copy-done.4, ...), custom_call_target="tpu_custom_call" | custom-call | tf_op jit(solution)/shard_map/early/pallas_call | solution.py:240
  147.4 1.3 copy-done
  149.7 12.2 %all-to-all-done = f32[64,1,2176]{2,1,0:T(1,128)} async-done(((f32[64,1,2176]{2,1,0:T(1,128)}), f32[64,1,2176]{2,1,0:T(1,128)}, u32[]{:S(2)}, u32[]{:S(2)}) %all-to-all-start) | async-done | bytes 557088 | tf_op jit(solution)/shard_map/all_to_all | solution.py:328
  161.9 5.2 %finish.1 = f32[8,512,128]{2,1,0:T(8,128)} custom-call(f32[1088,128]{1,0:T(8,128)} %bitcast.9.refs_0_, bf16[128,256]{1,0:T(8,128)(2,1)} %constant.36.clone.f1h.refs_1_, bf16[128,256]{1,0:T(8,128)(2,1)} %constant.37.clone.f1l.refs_2_, f32[2,128,128]{2,1,0:T(8,128)} %constant.41.clone.refs_3_, bf16[512,256]{1,0:T(8,128)(2,1)} %constant.42.clone.refs_4_, ...), custom_call_target="tpu_custom_call" | custom-call | tf_op jit(solution)/shard_map/finish/pallas_call | solution.py:298
  (44 shorter events, 7.5 us)
Async XLA Ops:
  0.0 1.6 copy-start.1
  1.6 3.2 %copy-start.11 = (s32[4,512]{1,0:T(4,128)S(1)}, s32[4,512]{1,0:T(4,128)}, u32[]{:S(2)}) copy-start(s32[4,512]{1,0:T(4,128)} %param.16) | copy-start | bytes 24580
  1.6 3.2 %copy-start.10 = (f32[8,4,512]{2,1,0:T(4,128)S(1)}, f32[8,4,512]{2,1,0:T(4,128)}, u32[]{:S(2)}) copy-start(f32[8,4,512]{2,1,0:T(4,128)} %param.17) | copy-start | bytes 196612
  1.6 3.3 %copy-start.12 = (s32[4,4]{1,0:T(4,128)S(1)}, s32[4,4]{1,0:T(4,128)}, u32[]{:S(2)}) copy-start(s32[4,4]{1,0:T(4,128)} %param.15) | copy-start | bytes 196
  2.2 7.3 %collective-permute-start.6 = (f32[1,136,256]{2,1,0:T(8,128)S(1)}, f32[1,136,256]{2,1,0:T(8,128)S(1)}, u32[]{:S(2)}, u32[]{:S(2)}) collective-permute-start(f32[1,136,256]{2,1,0:T(8,128)S(1)} %get-tuple-element.23.refs_3_), channel_id=1, source_target_pairs={{64,0},{128,64},{192,128},{256,192},{320,256},{384,320},{448,384},... | collective-permute-start | bytes 417800 | tf_op jit(solution)/shard_map/ppermute | solution.py:325
  3.5 15.1 %collective-permute-start.7 = (f32[1,376,256]{2,1,0:T(8,128)S(1)}, f32[1,376,256]{2,1,0:T(8,128)S(1)}, u32[]{:S(2)}, u32[]{:S(2)}) collective-permute-start(f32[1,376,256]{2,1,0:T(8,128)S(1)} %get-tuple-element.24.refs_4_), channel_id=1, source_target_pairs={{64,0},{128,64},{192,128},{256,192},{320,256},{384,320},{448,384},... | collective-permute-start | bytes 1155080 | tf_op jit(solution)/shard_map/ppermute | solution.py:325
  9.4 9.1 %collective-permute-start.8 = (f32[1,136,256]{2,1,0:T(8,128)S(1)}, f32[1,136,256]{2,1,0:T(8,128)S(1)}, u32[]{:S(2)}, u32[]{:S(2)}) collective-permute-start(f32[1,136,256]{2,1,0:T(8,128)S(1)} %collective-permute-done.6.refs_5_), channel_id=1, source_target_pairs={{64,0},{128,64},{192,128},{256,192},{320,256},{384,320},{448,384},... | collective-permute-start | bytes 417800 | tf_op jit(solution)/shard_map/ppermute | solution.py:325
  20.4 53.6 %all-to-all-start.1 = ((f32[64,1,2,8,128]{4,3,2,1,0:T(8,128)}), f32[64,1,2,8,128]{4,3,2,1,0:T(8,128)S(1)}, u32[]{:S(2)}, u32[]{:S(2)}) async-start(f32[64,1,2,8,128]{4,3,2,1,0:T(8,128)} %get-tuple-element.29), calls=%async_computation.1 | async-start | bytes 1048576 | tf_op jit(solution)/shard_map/all_to_all | solution.py:328
  34.8 37.1 %collective-permute-start.4 = (f32[2,376,256]{2,1,0:T(8,128)S(1)}, f32[2,376,256]{2,1,0:T(8,128)S(1)}, u32[]{:S(2)}, u32[]{:S(2)}) collective-permute-start(f32[2,376,256]{2,1,0:T(8,128)S(1)} %get-tuple-element.22.refs_4_), channel_id=1, source_target_pairs={{64,0},{128,64},{192,128},{256,192},{320,256},{384,320},{448,384},... | collective-permute-start | bytes 2310152 | tf_op jit(solution)/shard_map/ppermute | solution.py:325
  36.1 25.8 %collective-permute-start.3 = (f32[2,136,256]{2,1,0:T(8,128)S(1)}, f32[2,136,256]{2,1,0:T(8,128)S(1)}, u32[]{:S(2)}, u32[]{:S(2)}) collective-permute-start(f32[2,136,256]{2,1,0:T(8,128)S(1)} %get-tuple-element.21.refs_3_), channel_id=1, source_target_pairs={{64,0},{128,64},{192,128},{256,192},{320,256},{384,320},{448,384},... | collective-permute-start | bytes 835592 | tf_op jit(solution)/shard_map/ppermute | solution.py:325
  61.9 10.0 %collective-permute-start.5 = (f32[2,136,256]{2,1,0:T(8,128)S(1)}, f32[2,136,256]{2,1,0:T(8,128)S(1)}, u32[]{:S(2)}, u32[]{:S(2)}) collective-permute-start(f32[2,136,256]{2,1,0:T(8,128)S(1)} %collective-permute-done.3.refs_5_), channel_id=1, source_target_pairs={{64,0},{128,64},{192,128},{256,192},{320,256},{384,320},{448,384},... | collective-permute-start | bytes 835592 | tf_op jit(solution)/shard_map/ppermute | solution.py:325
  74.0 53.6 %all-to-all-start.2 = ((f32[64,2,2,8,128]{4,3,2,1,0:T(8,128)}), f32[64,2,2,8,128]{4,3,2,1,0:T(8,128)S(1)}, u32[]{:S(2)}, u32[]{:S(2)}) async-start(f32[64,2,2,8,128]{4,3,2,1,0:T(8,128)} %get-tuple-element.30), calls=%async_computation.2 | async-start | bytes 2097152 | tf_op jit(solution)/shard_map/all_to_all | solution.py:328
  85.6 58.0 %copy-start.3 = (bf16[128,256]{1,0:T(8,128)(2,1)S(1)}, bf16[128,256]{1,0:T(8,128)(2,1)}, u32[]{:S(2)}) copy-start(bf16[128,256]{1,0:T(8,128)(2,1)} %constant.37.clone.f1l.refs_2_) | copy-start | bytes 196612
  85.6 58.0 %copy-start.4 = (bf16[128,256]{1,0:T(8,128)(2,1)S(1)}, bf16[128,256]{1,0:T(8,128)(2,1)}, u32[]{:S(2)}) copy-start(bf16[128,256]{1,0:T(8,128)(2,1)} %constant.36.clone.f1h.refs_1_) | copy-start | bytes 196612
  85.6 58.0 %copy-start.5 = (bf16[512,256]{1,0:T(8,128)(2,1)S(1)}, bf16[512,256]{1,0:T(8,128)(2,1)}, u32[]{:S(2)}) copy-start(bf16[512,256]{1,0:T(8,128)(2,1)} %constant.40.clone.ml) | copy-start | bytes 786436
  85.6 58.0 %copy-start.6 = (bf16[512,256]{1,0:T(8,128)(2,1)S(1)}, bf16[512,256]{1,0:T(8,128)(2,1)}, u32[]{:S(2)}) copy-start(bf16[512,256]{1,0:T(8,128)(2,1)} %constant.39.clone.mh) | copy-start | bytes 786436
  85.6 58.0 %copy-start.7 = (f32[2,128,128]{2,1,0:T(8,128)S(1)}, f32[2,128,128]{2,1,0:T(8,128)}, u32[]{:S(2)}) copy-start(f32[2,128,128]{2,1,0:T(8,128)} %constant.38.clone.turn) | copy-start | bytes 393220
  85.6 58.0 %copy-start.8 = (bf16[128,256]{1,0:T(8,128)(2,1)S(1)}, bf16[128,256]{1,0:T(8,128)(2,1)}, u32[]{:S(2)}) copy-start(bf16[128,256]{1,0:T(8,128)(2,1)} %constant.35.clone.f0l) | copy-start | bytes 196612
  85.7 24.5 %collective-permute-start.1 = (f32[1,376,256]{2,1,0:T(8,128)S(1)}, f32[1,376,256]{2,1,0:T(8,128)S(1)}, u32[]{:S(2)}, u32[]{:S(2)}) collective-permute-start(f32[1,376,256]{2,1,0:T(8,128)S(1)} %get-tuple-element.20.refs_4_), channel_id=1, source_target_pairs={{64,0},{128,64},{192,128},{256,192},{320,256},{384,320},{448,384},... | collective-permute-start | bytes 1155080 | tf_op jit(solution)/shard_map/ppermute | solution.py:325
  87.1 15.8 %collective-permute-start = (f32[1,136,256]{2,1,0:T(8,128)S(1)}, f32[1,136,256]{2,1,0:T(8,128)S(1)}, u32[]{:S(2)}, u32[]{:S(2)}) collective-permute-start(f32[1,136,256]{2,1,0:T(8,128)S(1)} %get-tuple-element.19.refs_3_), channel_id=1, source_target_pairs={{64,0},{128,64},{192,128},{256,192},{320,256},{384,320},{448,384},... | collective-permute-start | bytes 417800 | tf_op jit(solution)/shard_map/ppermute | solution.py:325
  102.8 7.3 %collective-permute-start.2 = (f32[1,136,256]{2,1,0:T(8,128)S(1)}, f32[1,136,256]{2,1,0:T(8,128)S(1)}, u32[]{:S(2)}, u32[]{:S(2)}) collective-permute-start(f32[1,136,256]{2,1,0:T(8,128)S(1)} %collective-permute-done.refs_5_), channel_id=1, source_target_pairs={{64,0},{128,64},{192,128},{256,192},{320,256},{384,320},{448,384},... | collective-permute-start | bytes 417800 | tf_op jit(solution)/shard_map/ppermute | solution.py:325
  127.6 34.3 %all-to-all-start = ((f32[64,1,2176]{2,1,0:T(1,128)}), f32[64,1,2176]{2,1,0:T(1,128)}, u32[]{:S(2)}, u32[]{:S(2)}) async-start(f32[64,1,2176]{2,1,0:T(1,128)} %bitcast.8), calls=%async_computation | async-start | bytes 1114112 | tf_op jit(solution)/shard_map/all_to_all | solution.py:328
  147.4 1.4 copy-start
  148.7 1.0 copy-start.2
  (1 other events, 0.8 us)
